TPU v7x, 8 devices: a whole 2x2x1 slice. The times are simulated.
8 devices in a mesh: dp: 2 (over z, y), tp: 4 (over x, core).
Axes of the slice: x: 2, y: 2, z: 1, core: 2. Of those that a mesh axis runs over, the one named last changes fastest.
Arguments:
- hidden: bfloat16 [16384, 4096], P(('dp', 'tp')), parts along dimension 0
- ln_gain: float32 [4096], replicated
- ln_bias: float32 [4096], replicated
- embed: bfloat16 [8192, 4096], P('tp')
- targets: int32 [16384], P(('dp', 'tp')), parts along dimension 0
- loss_mask: int32 [16384], P(('dp', 'tp')), parts along dimension 0
Outputs:
- output 1: float32 [16384], P(('dp', 'tp')), parts along dimension 0
- output 2: float32 [2], P('dp'), parts along dimension 0
- output 3: bfloat16 [16384, 4096], P(('dp', 'tp')), parts along dimension 0
- output 4: float32 [16384, 4096], P(('dp', 'tp')), parts along dimension 0
- output 5: float32 [8192], P('dp'), parts along dimension 0
- output 6: float32 [8192], P('dp'), parts along dimension 0
There are 2 independent parts. A program takes and returns all parts, laid end to end along the dimension named above; an argument that names none is the same for every part.
All inputs are finite; a program needn't handle non-finite values.
Results may differ from a plain program's by a relative error of at most 0.001.
Values are sent between devices in bfloat16 or wider.
A program may use at most 1 GiB of HBM per device.

v0:
```python
import jax
import jax.numpy as jnp
from jax import lax
from jax.sharding import PartitionSpec as P

LN_EPS = 1e-5


def layer_norm(hidden, ln_gain, ln_bias):
    h_f32 = hidden.astype(jnp.float32)
    centred = h_f32 - jnp.mean(h_f32, axis=-1, keepdims=True)
    inv_std = lax.rsqrt(jnp.mean(centred * centred, axis=-1, keepdims=True) + LN_EPS)
    x_hat = centred * inv_std
    return x_hat, inv_std, (x_hat * ln_gain + ln_bias).astype(jnp.bfloat16)


def norm_backward(d_normed, x_hat, inv_std, ln_gain):
    value_a6 = d_normed * ln_gain
    centre_term = jnp.mean(value_a6, axis=-1, keepdims=True)
    proj_term = jnp.mean(value_a6 * x_hat, axis=-1, keepdims=True)
    return (inv_std * (value_a6 - centre_term - x_hat * proj_term)).astype(jnp.bfloat16)


def solution(mesh):
    group = mesh.shape['tp']

    def body(hidden, ln_gain, ln_bias, embed, targets, loss_mask):
        tokens = hidden.shape[0]
        shard_vocab = embed.shape[0]
        rank = lax.axis_index('tp')
        x_hat, inv_std, normed = layer_norm(hidden, ln_gain, ln_bias)
        gathered = lax.all_gather(normed, 'tp', tiled=True)
        all_targets = lax.all_gather(targets, 'tp', tiled=True)
        all_weights = lax.all_gather(loss_mask, 'tp', tiled=True).astype(jnp.float32)
        count = lax.psum(jnp.sum(loss_mask.astype(jnp.float32)), 'tp')
        logits = jnp.einsum('sd,vd->sv', gathered, embed, preferred_element_type=jnp.float32)
        vocab_ids = rank * shard_vocab + lax.broadcasted_iota(jnp.int32, (1, shard_vocab), 1)
        onehot = vocab_ids == all_targets[:, None]
        local_max = jnp.max(logits, axis=-1)
        local_sum = jnp.sum(jnp.exp(logits - local_max[:, None]), axis=-1)
        local_target = jnp.sum(jnp.where(onehot, logits, 0.0), axis=-1)
        global_max = lax.pmax(local_max, 'tp')
        combined = lax.psum(jnp.stack([local_sum * jnp.exp(local_max - global_max), local_target]), 'tp')
        log_norm = global_max + jnp.log(combined[0])
        all_loss = (log_norm - combined[1]) * all_weights
        mean_loss = jnp.sum(all_loss) / count
        d_logits = ((jnp.exp(logits - log_norm[:, None]) - onehot.astype(jnp.float32)) * (all_weights / count)[:, None]).astype(jnp.bfloat16)
        d_embed = jnp.einsum('sv,sd->vd', d_logits, gathered, preferred_element_type=jnp.float32)
        d_part = jnp.einsum('sv,vd->sd', d_logits, embed, preferred_element_type=jnp.float32)
        d_normed = lax.psum_scatter(d_part, 'tp', scatter_dimension=0, tiled=True)
        norm_grads = lax.psum(jnp.stack([jnp.sum(d_normed * x_hat, axis=0), jnp.sum(d_normed, axis=0)]), 'tp')
        d_hidden = norm_backward(d_normed, x_hat, inv_std, ln_gain)
        own_loss = all_loss.reshape(group, tokens)[rank]
        return own_loss, mean_loss.reshape(1), d_hidden, d_embed, norm_grads[0], norm_grads[1]

    token_rows = P(('dp', 'tp'))
    token_mat = P(('dp', 'tp'), None)
    return jax.shard_map(body, mesh=mesh, in_specs=(token_mat, P(), P(), P('tp', None), token_rows, token_rows), out_specs=(token_rows, P('dp'), token_mat, token_mat, P('dp'), P('dp')), check_vma=False)
```

profile of v0, /device:TPU:0, one launch (start us, length us, event | category | flops | bytes accessed | tf_op | source)
XLA Modules:
  0.0 1737.0 jit_solution(7187372510684941166)
XLA Ops:
  7.2 0.0 copy-start.2
  7.2 0.0 copy-start.10
  7.2 0.0 all-gather.2.cloned.1.call-start
  7.2 0.0 slice-start
  7.2 0.0 slice-start.1
  7.3 8.5 convert_reduce_fusion
  15.8 0.0 copy-start
  15.8 0.0 slice-start.2
  15.8 0.0 slice-start.3
  15.8 0.0 copy-start.11
  15.8 9.3 fusion.17
  25.1 0.0 copy-done
  25.1 0.0 copy-start.4
  25.1 0.6 copy-done.4
  25.7 0.0 copy-done.2
  25.7 0.0 copy-done.10
  25.7 0.0 slice-done
  25.7 0.0 slice-done.1
  25.7 0.0 slice-done.2
  25.8 0.0 slice-done.3
  25.8 11.0 fusion.11
  36.7 0.0 all-gather.2.cloned.1.call-update
  36.8 0.0 all-reduce.3.cloned.1.call-start
  36.8 0.0 copy-done.11
  36.8 10.0 all_gather.10
  46.8 0.6 iota_add_fusion
  47.4 382.0 %all-gather.2.cloned.1.call-done = bf16[8192,4096]{1,0:T(8,128)(2,1)} async-done(((bf16[2048,4096]{1,0:T(8,128)(2,1)}), bf16[8192,4096]{1,0:T(8,128)(2,1)}) %all-gather.2.cloned.1.call-update) | async-done | bytes 67108880 | tf_op jit(solution)/shard_map/all_gather | solution.py:32
  429.4 0.0 copy-start.6
  429.4 0.0 copy-start.8
  429.4 149.5 %fusion.24 = (f32[8192]{0:T(1024)S(1)}, f32[8192,2048]{0,1:T(8,128)}) fusion(bf16[8192,4096]{1,0:T(8,128)(2,1)} %all-gather.2.cloned.1.call-done, bf16[2048,4096]{1,0:T(8,128)(2,1)} %param.9), kind=kOutput, calls=%fused_computation.41 | convolution fusion | flops 137455730688 | bytes 151027712 | tf_op jit(solution)/shard_map/sd,vd->sv/dot_general | solution.py:36
  579.0 10.4 pmax.7
  589.3 0.0 copy-done.6
  589.4 0.0 copy-done.8
  589.4 0.0 copy-start.9
  589.4 21.5 %exponential_reduce_fusion = (f32[8192]{0:T(1024)S(1)}, f32[8192]{0:T(1024)S(1)}) fusion(f32[8192,2048]{0,1:T(8,128)} %get-tuple-element.21, f32[8192]{0:T(1024)S(1)} %get-tuple-element.20, s32[8192]{0:T(1024)S(1)} %copy-done.6, s32[2048]{0:T(1024)S(1)} %copy-done.8), kind=kLoop, calls=%fused_computation.6 | loop fusion | flops 83869696 | bytes 67248128 | tf_op jit(solution)/shard_map/reduce_sum | solution.py:40
  610.9 0.7 pad_maximum_fusion
  611.6 0.0 all-reduce.3.cloned.1.call-update
  611.6 0.0 reduce-scatter.4.cloned.1.call-start
  611.7 0.0 copy-done.9
  611.7 0.6 convert_reduce_fusion.1
  612.3 6.4 psum.22
  618.6 8.4 all_gather.11
  627.1 11.7 all-reduce.3.cloned.1.call-done
  638.8 1.0 slice_log_fusion
  639.8 1.9 fusion.22
  641.7 159.7 %fusion.20 = f32[8192,4096]{1,0:T(8,128)} fusion(bf16[2048,4096]{1,0:T(8,128)(2,1)} %param.9, f32[8192,2048]{0,1:T(8,128)} %get-tuple-element.21, f32[8192]{0:T(1024)S(1)} %get-tuple-element.19, f32[8192]{0:T(1024)S(1)} %get-tuple-element.14, s32[8192]{0:T(1024)S(1)} %copy-done.6, s32[2048]{0:T(1024)S(1)} %copy-done.8), kind=kOutput, calls=%fused_computation.38 | convolution fusion | flops 137539616768 | bytes 218210304 | tf_op jit(solution)/shard_map/sv,vd->sd/dot_general | solution.py:49
  801.3 0.0 copy-start.7
  801.3 0.0 reduce-scatter.4.cloned.1.call-update
  802.7 0.0 copy-done.7
  802.7 0.6 constant_dynamic-slice_fusion
  803.3 0.0 copy-start.1
  803.3 0.0 copy-start.3
  803.4 0.0 copy-start.5
  803.4 165.5 %fusion.18 = f32[2048,4096]{1,0:T(8,128)} fusion(bf16[8192,4096]{1,0:T(8,128)(2,1)} %all-gather.2.cloned.1.call-done, f32[8192,2048]{0,1:T(8,128)} %get-tuple-element.21, f32[8192]{0:T(1024)S(1)} %get-tuple-element.19, f32[8192]{0:T(1024)S(1)} %get-tuple-element.14, s32[8192]{0:T(1024)S(1)} %copy-done.6, s32[2048]{0:T(1024)S(1)} %copy-done.8), kind=kOutput, calls=%fused_computation.37 | convolution fusion | flops 137539616768 | bytes 167878656 | tf_op jit(solution)/shard_map/sv,sd->vd/dot_general | solution.py:48
  968.9 702.2 %reduce-scatter.4.cloned.1.call-done = f32[2048,4096]{1,0:T(8,128)} async-done(((f32[8192,4096]{1,0:T(8,128)}), f32[2048,4096]{1,0:T(8,128)}) %reduce-scatter.4.cloned.1.call-update) | async-done | bytes 33554448
  1671.1 0.0 copy-done.1
  1671.1 0.0 copy-done.3
  1671.2 0.0 copy-done.5
  1671.2 21.5 %fusion.16 = (f32[4096]{0:T(1024)S(1)}, f32[2048]{0:T(1024)S(1)}, f32[2048]{0:T(1024)S(1)}, f32[4096]{0:T(1024)S(1)}) fusion(f32[2048,4096]{1,0:T(8,128)} %reduce-scatter.4.cloned.1.call-done, bf16[2048,4096]{1,0:T(8,128)(2,1)} %param.6, f32[2048]{0:T(1024)S(1)} %copy-done.5, f32[2048]{0:T(1024)S(1)} %copy-done.1, f32[4096]{0:T(1024)S(1)} %copy-done.3), kind=kLoop, calls=%fused_computation.21 | loop fusion | flops 83873792 | bytes 50413568 | tf_op jit(solution)/shard_map/reduce_sum | solution.py:51
  1692.7 10.3 psum.23
  1702.9 0.6 fusion.23
  1703.6 25.7 %fusion.15 = bf16[2048,4096]{1,0:T(8,128)(2,1)} fusion(bf16[2048,4096]{1,0:T(8,128)(2,1)} %param.6, f32[2048,4096]{1,0:T(8,128)} %reduce-scatter.4.cloned.1.call-done, f32[2048]{0:T(1024)S(1)} %get-tuple-element.22, f32[2048]{0:T(1024)S(1)} %get-tuple-element.23, f32[4096]{0:T(1024)S(1)} %copy-done.3, f32[2048]{0:T(1024)S(1)} %copy-done.5, f32[2048]{0:T(1024)S(1)} %copy-done.1), kind=kLoop, calls=%fused_computation.20 | loop fusion | flops 75497472 | bytes 67158016 | tf_op jit(solution)/shard_map/convert_element_type | solution.py:21
  (7 shorter events, 0.1 us)
Async XLA Ops:
  7.2 18.6 %copy-start.2 = (f32[4096]{0:T(1024)S(1)}, f32[4096]{0:T(1024)}, u32[]{:S(2)}) copy-start(f32[4096]{0:T(1024)} %param.7) | copy-start | bytes 49156
  7.2 18.6 %copy-start.10 = (f32[4096]{0:T(1024)S(1)}, f32[4096]{0:T(1024)}, u32[]{:S(2)}) copy-start(f32[4096]{0:T(1024)} %param.8) | copy-start | bytes 49156
  7.2 422.2 %all-gather.2.cloned.1.call-start = ((), (), s32[]{:S(2)}) async-start(), calls=%async_computation.1 | async-start | bytes 83886080 | tf_op jit(solution)/shard_map/all_gather | solution.py:32
  7.2 18.5 %slice-start = ((s8[16777216]{0:T(1024)(128)(4,1)}), s8[4194304]{0:T(1024)(128)(4,1)S(1)}, s32[]{:S(2)}) async-start(s8[16777216]{0:T(1024)(128)(4,1)} %bitcast.17), calls=%async_computation.4 | async-start | bytes 8388608
  7.2 18.5 %slice-start.1 = ((s8[16777216]{0:T(1024)(128)(4,1)}), s8[4194304]{0:T(1024)(128)(4,1)S(1)}, s32[]{:S(2)}) async-start(s8[16777216]{0:T(1024)(128)(4,1)} %bitcast.17), calls=%async_computation.5 | async-start | bytes 8388608
  15.8 9.4 copy-start
  15.8 10.0 slice-start.2
  15.8 10.0 slice-start.3
  15.8 21.0 %copy-start.11 = (s32[2048]{0:T(1024)S(1)}, s32[2048]{0:T(1024)}, u32[]{:S(2)}) copy-start(s32[2048]{0:T(1024)} %param.10) | copy-start | bytes 24580
  25.1 0.6 copy-start.4
  36.8 602.0 %all-reduce.3.cloned.1.call-start = ((), (), s32[]{:S(2)}) async-start(), calls=%async_computation.2 | async-start | bytes 131072 | tf_op jit(solution)/shard_map/psum | solution.py:43
  429.4 159.9 %copy-start.6 = (s32[8192]{0:T(1024)S(1)}, s32[8192]{0:T(1024)}, u32[]{:S(2)}) copy-start(s32[8192]{0:T(1024)} %all_gather.10) | copy-start | bytes 98308
  429.4 159.9 %copy-start.8 = (s32[2048]{0:T(1024)S(1)}, s32[2048]{0:T(1024)}, u32[]{:S(2)}) copy-start(s32[2048]{0:T(1024)} %iota_add_fusion) | copy-start | bytes 24580
  589.4 22.3 %copy-start.9 = (s32[2048]{0:T(1024)S(1)}, s32[2048]{0:T(1024)}, u32[]{:S(2)}) copy-start(s32[2048]{0:T(1024)} %param.11) | copy-start | bytes 24580
  611.6 1059.5 %reduce-scatter.4.cloned.1.call-start = ((), (), s32[]{:S(2)}) async-start(), calls=%async_computation.3 | async-start | bytes 167772160
  801.3 1.4 copy-start.7
  803.3 867.8 %copy-start.1 = (f32[2048]{0:T(1024)S(1)}, f32[2048]{0:T(1024)}, u32[]{:S(2)}) copy-start(f32[2048]{0:T(1024)} %copy-done) | copy-start | bytes 24580
  803.3 867.8 %copy-start.3 = (f32[4096]{0:T(1024)S(1)}, f32[4096]{0:T(1024)}, u32[]{:S(2)}) copy-start(f32[4096]{0:T(1024)} %param.7) | copy-start | bytes 49156
  803.4 867.8 %copy-start.5 = (f32[2048]{0:T(1024)S(1)}, f32[2048]{0:T(1024)}, u32[]{:S(2)}) copy-start(f32[2048]{0:T(1024)} %copy-done.4) | copy-start | bytes 24580
Sparse Core Ops, SparseCore 0:
  36.9 392.4 all-gather.1
  611.8 27.0 all-reduce.2
  801.5 869.6 reduce-scatter.3
where the time goes:
time: 1740 us
  waiting for transfers between devices  1100 us (63%)
  matrix products  475 us (27%)
  other arithmetic  101 us (6%)
  blocking collectives  45.4 us (3%)
    unnamed x4, waiting for transfers between devices  702 us
    all_gather x1, waiting for transfers between devices, body(): gathered = lax.all_gather(normed, 'tp', tiled=True)  382 us
    dot_general x1, matrix products, body(): jnp.einsum('sv,sd->vd', d_logits, gathered, preferred_element_type=jnp.fl...  166 us
    dot_general x1, matrix products, body(): jnp.einsum('sv,vd->sd', d_logits, embed, preferred_element_type=jnp.float32)  160 us
    dot_general x1, matrix products, body(): jnp.einsum('sd,vd->sv', gathered, embed, preferred_element_type=jnp.float32)  150 us
  transfers between devices with their start and end apart: 3, of which 3 were waited for; matrix products, arithmetic and copies ran while one was open for 10% of the time, Pallas kernels for 0%

commit v1 on v0

v1 whole, which is shorter than its diff:
```python
import functools

import jax
import jax.numpy as jnp
from jax import lax
from jax.experimental import pallas as pl
from jax.experimental.pallas import tpu as pltpu
from jax.sharding import PartitionSpec as P

LN_EPS = 1e-5
LOWEST = float(jnp.finfo(jnp.float32).min)

TOK = 2048
ROWS = 2048
DIM = 4096
VOCAB = 8192
TILE = 512
TILES = VOCAB // TILE
HB = 1024
HBS = TOK // HB
CHUNK = 64
CHUNKS = ROWS // 2 // CHUNK
LN_ROWS = 256
STAT_ROWS = 16
LN_UNROLL = 4
XCH = 256
XCHS = TOK // XCH
KT = 512
DEFER = 6
WAIT_STEP = {2: 0, 6: 1, 10: 2, 15: 3}
ZB = 512
NCOL = 512
KCOL = 1024
NB_UNROLL = 8
GROUPS = TOK // 128
NT = (((1,), (1,)), ((), ()))


def peers():
    dp, tp = lax.axis_index('dp'), lax.axis_index('tp')
    core = lax.rem(tp, 2)
    pair = tp - core
    other = 2 - pair
    part = pair + 1 - core
    return dp, tp, (dp, part), (dp, other + core), (dp, other + 1 - core), (1 - dp, tp)


def remote(src, dst, ssem, rsem, dev):
    return pltpu.make_async_remote_copy(
        src_ref=src, dst_ref=dst, send_sem=ssem, recv_sem=rsem, device_id=dev, device_id_type=pl.DeviceIdType.MESH)


def spread(row, rows, dst):
    dst[rows, :] = jnp.transpose(jnp.broadcast_to(row, (128, 128)))


def step_kernel(hid, gain, bias, emb, tcol, info,
                e_all, x_out, z_out, stat_all, info_all, lse_b, mean_b, rstd_b,
                dhid, x_part, x_xp, x_xq, dzt_own, dzt_out, dzt_part, dzt_last, de_part, gsum_all,
                info_v, stat_v, stats, infos, gb_v, gs_v, g8,
                h_sem, xo_sem, e_sem, eo_sem, z_sem, small_sem, wide_sem, dzo_sem, big_sem, g_sem,
                xs_send, ys_send, ds_send, pe_send, sm_send, xt_send, xd_send, xp_send, dz_send, g_send,
                x_recv, y_recv, d_recv, pe_recv, info_recv, stat_recv, xt_recv, xd_recv, xp_recv, dz_recv, g_recv):
    dp, tp, part, xp, xq, yp = peers()
    core = lax.rem(tp, 2)
    xp_rank = 2 - (tp - core) + core
    xq_rank = 2 - (tp - core) + 1 - core
    group = ((1, part), (2, xp), (3, xq))
    barrier = pltpu.get_barrier_semaphore()
    for dev in (part, xp, xq, yp):
        pl.semaphore_signal(barrier, inc=1, device_id=dev, device_id_type=pl.DeviceIdType.MESH)
    pl.semaphore_wait(barrier, 4)

    def xrows(ref, j):
        return ref.at[pl.ds(pl.multiple_of(j * XCH, XCH), XCH)]

    def xt_copy(j):
        return remote(xrows(x_out, j), xrows(x_xp, j), xt_send, xt_recv.at[j], xp)

    def xd_copy(j):
        return remote(xrows(x_xp, j), xrows(x_xq, j), xd_send, xd_recv.at[j], part)

    def xt_event(j):
        xt_copy(j).wait_recv()
        xd_copy(j).start()
    xp_copy = remote(x_out, x_part, xp_send, xp_recv, part)

    def forward(xs, hbuf, ebuf, z0, z1, tc_v, m_s, s_s, t_s, mr_v, gb8):
        def tile_row(j):
            return ROWS * 2 + (j // 2) * TILE + lax.rem(j, 2) * CHUNK

        def x_copy(j):
            src = emb.at[pl.ds(pl.multiple_of(dp * (ROWS // 2) + j * CHUNK, CHUNK), CHUNK)]
            return remote(src, e_all.at[pl.ds(pl.multiple_of(tile_row(j), CHUNK), CHUNK)], xs_send, x_recv.at[j], xp)

        def piece(j, p):
            return e_all.at[pl.ds(pl.multiple_of(tile_row(j) + p * 2 * CHUNK, CHUNK), CHUNK)]

        def y_copy(j):
            return remote(piece(j, 0), piece(j, 1), ys_send, y_recv.at[j], yp)

        def d_copy(j, p):
            return remote(piece(j, p), piece(j, p + 2), ds_send, d_recv.at[j // 2], part)

        def pe_copy(i):
            return remote(emb.at[pl.ds(pl.multiple_of(i * TILE, TILE), TILE)],
                          e_all.at[pl.ds(pl.multiple_of(ROWS + i * TILE, TILE), TILE)], pe_send, pe_recv.at[i], part)

        cp = pltpu.make_async_copy(info, info_v, small_sem.at[0])
        cp.start()

        def h_copy(i):
            return pltpu.make_async_copy(hid.at[pl.ds(pl.multiple_of(i * LN_ROWS, LN_ROWS), LN_ROWS)], hbuf.at[lax.rem(i, 2)], h_sem.at[lax.rem(i, 2)])
        h_copy(0).start()

        for p, dev in group:
            remote(info, info_all.at[tp], sm_send, info_recv.at[p], dev).start()

        def start_x(j, c):
            x_copy(j).start()
            return c
        lax.fori_loop(0, CHUNKS, start_x, 0)

        def start_pe(i, c):
            pe_copy(i).start()
            return c
        lax.fori_loop(0, ROWS // TILE, start_pe, 0)

        def e_load(t):
            slot = lax.rem(t, 2)
            return pltpu.make_async_copy(e_all.at[pl.ds(pl.multiple_of(t * TILE, TILE), TILE)], ebuf.at[slot], e_sem.at[slot])

        def e_load_own(t):
            slot = lax.rem(t, 2)
            return pltpu.make_async_copy(emb.at[pl.ds(pl.multiple_of(t * TILE, TILE), TILE)], ebuf.at[slot], e_sem.at[slot])
        e_load_own(0).start()

        cp.wait()
        pltpu.make_async_copy(info_v, info_all.at[tp], small_sem.at[0]).start()
        gb8[0] = jnp.broadcast_to(gain[...], (8, DIM))
        gb8[1] = jnp.broadcast_to(bias[...], (8, DIM))

        def ln_tile(i, c):
            slot = lax.rem(i, 2)

            @pl.when(i + 1 < TOK // LN_ROWS)
            def _():
                h_copy(i + 1).start()
            h_copy(i).wait()

            def ln_rows(r, c2):
                base = r * LN_UNROLL * 16

                def at(u):
                    return pl.ds(pl.multiple_of(base + u * 16, 16), 16)

                def part_of(u, k):
                    return hbuf[slot, at(u), k * 128:(k + 1) * 128].astype(jnp.float32)
                means, rstds = [], []
                for u in range(LN_UNROLL):
                    tot = part_of(u, 0)
                    for k in range(1, DIM // 128):
                        tot = tot + part_of(u, k)
                    means.append(jnp.broadcast_to(jnp.sum(tot, axis=-1, keepdims=True) * (1.0 / DIM), (16, 128)))
                for u in range(LN_UNROLL):
                    tot = jnp.zeros((16, 128), jnp.float32)
                    for k in range(DIM // 128):
                        diff = part_of(u, k) - means[u]
                        tot = tot + diff * diff
                    var = jnp.sum(tot, axis=-1, keepdims=True) * (1.0 / DIM)
                    rstds.append(jnp.broadcast_to(lax.rsqrt(var + LN_EPS), (16, 128)))
                for u in range(LN_UNROLL):
                    row = pl.ds(pl.multiple_of(i * LN_ROWS + base + u * 16, 16), 16)
                    mr_v[0, row, :] = means[u]
                    mr_v[1, row, :] = rstds[u]
                    for k in range(DIM // 128):
                        cols = slice(k * 128, (k + 1) * 128)
                        g2 = jnp.concatenate([gb8[0, :, cols]] * 2, axis=0)
                        b2 = jnp.concatenate([gb8[1, :, cols]] * 2, axis=0)
                        xs[row, cols] = ((part_of(u, k) - means[u]) * rstds[u] * g2 + b2).astype(jnp.bfloat16)
                return c2
            lax.fori_loop(0, LN_ROWS // (16 * LN_UNROLL), ln_rows, 0)
            rows = pl.ds(pl.multiple_of(i * LN_ROWS, LN_ROWS), LN_ROWS)
            pltpu.make_async_copy(xs.at[rows], x_out.at[rows], xo_sem).start()
            return c
        lax.fori_loop(0, TOK // LN_ROWS, ln_tile, 0)

        for i, dst in enumerate((mean_b, rstd_b)):
            pltpu.make_async_copy(mr_v.at[i], dst, wide_sem.at[i + 1]).start()
        m_s[...] = jnp.full((TOK, 128), LOWEST, jnp.float32)
        s_s[...] = jnp.zeros((TOK, 128), jnp.float32)
        t_s[...] = jnp.zeros((TOK, 128), jnp.float32)
        for r in range(GROUPS):
            spread(tcol[r:r + 1, :], slice(r * 128, (r + 1) * 128), tc_v)
        z1[...] = jnp.full((HB, TILE), LOWEST, jnp.float32)

        zs = (z0, z1)

        def product(t, h):
            zs[h][...] = lax.dot_general(xs[h * HB:(h + 1) * HB, :], ebuf[lax.rem(t, 2)], NT, preferred_element_type=jnp.float32)

        def statistics(t, h):
            z = zs[h]
            lane = lax.broadcasted_iota(jnp.int32, (STAT_ROWS, 128), 1)
            for r in range(0, HB, STAT_ROWS):
                rows = slice(h * HB + r, h * HB + r + STAT_ROWS)
                zk = [z[r:r + STAT_ROWS, k * 128:(k + 1) * 128] for k in range(TILE // 128)]
                old = m_s[rows, :]
                new = jnp.maximum(jnp.maximum(jnp.maximum(zk[0], zk[1]), jnp.maximum(zk[2], zk[3])), old)
                tot = s_s[rows, :] * jnp.exp(old - new)
                tgt = t_s[rows, :]
                diff = tc_v[rows, :] - t * TILE
                for k in range(TILE // 128):
                    tot = tot + jnp.exp(zk[k] - new)
                    tgt = tgt + jnp.where(diff == lane + k * 128, zk[k], 0.0)
                m_s[rows, :] = new
                s_s[rows, :] = tot
                t_s[rows, :] = tgt

        def z_copy(t, h):
            return pltpu.make_async_copy(
                zs[h], z_out.at[pl.ds(h * HB, HB), pl.ds(pl.multiple_of(t * TILE, TILE), TILE)], z_sem.at[h])

        def x_event(j):
            x_copy(j).wait_recv()
            y_copy(j).start()
            d_copy(j, 0).start()

        def y_event(j):
            y_copy(j).wait_recv()
            d_copy(j, 1).start()

        def p_event(k):
            rows = e_all.at[pl.ds(pl.multiple_of(2 * ROWS + k * TILE + TILE // 2, TILE // 2), TILE // 2)]
            pltpu.make_async_copy(rows, rows, d_recv.at[k]).wait()
            e_load(8 + k).start()

        half_tiles = TILES // 2

        def start_events(t):
            @pl.when(t < TILES - 1)
            def _():
                x_event(t)

            @pl.when(t == TILES - 2)
            def _():
                xt_copy(0).start()
                y_event(TILES - 3)
                p_event(6)

            @pl.when(t == TILES - 1)
            def _():
                y_event(TILES - 2)
                y_event(TILES - 1)
                p_event(7)
            e_load(t).wait()

            @pl.when(t < 4)
            def _():
                slot = lax.rem(t, 2)
                pltpu.make_async_copy(ebuf.at[slot], e_all.at[pl.ds(pl.multiple_of(t * TILE, TILE), TILE)], eo_sem.at[slot]).start()

        def middle_events(t):
            @pl.when((t >= 1) & (t < TILES - 2))
            def _():
                y_event(t - 1)

            @pl.when((t >= 1) & (t < 5))
            def _():
                slot = lax.rem(t - 1, 2)
                pltpu.make_async_copy(ebuf.at[slot], e_all.at[pl.ds(0, TILE)], eo_sem.at[slot]).wait()

            @pl.when(t == 8)
            def _():
                pltpu.make_async_copy(xs, x_out, xo_sem).wait()

            @pl.when(t < 3)
            def _():
                e_load_own(t + 1).start()

            @pl.when((t >= 3) & (t < 7))
            def _():
                pe_copy(t - 3).wait_recv()
                e_load(t + 1).start()

            @pl.when((t >= half_tiles - 1) & (t < TILES - 3))
            def _():
                p_event(t - (half_tiles - 1))

            @pl.when(t == TILES - 2)
            def _():
                x_event(TILES - 1)

        def step(t, c):
            @pl.when(t > 0)
            def _():
                z_copy(t - 1, 1).start()
            start_events(t)

            @pl.when(t > 0)
            def _():
                z_copy(t - 1, 0).wait()
            statistics(t - 1, 1)
            product(t, 0)
            z_copy(t, 0).start()
            middle_events(t)

            @pl.when(t > 0)
            def _():
                z_copy(t - 1, 1).wait()
            statistics(t, 0)
            product(t, 1)
            return c
        last = TILES - 1
        lax.fori_loop(0, TILES, step, 0)
        z_copy(last, 1).start()
        statistics(last, 1)

        def finish(i, c):
            for u in range(4):
                r = i * 4 + u
                rows = pl.ds(pl.multiple_of(r * 128, 128), 128)
                m = m_s[rows, :]
                top = jnp.max(m, axis=-1, keepdims=True)
                tot = jnp.sum(s_s[rows, :] * jnp.exp(m - top), axis=-1, keepdims=True)
                lse = jnp.broadcast_to(top + jnp.log(tot), (128, 128))
                tgt = jnp.broadcast_to(jnp.sum(t_s[rows, :], axis=-1, keepdims=True), (128, 128))
                m_s[rows, :] = lse
                stat_v[0, pl.ds(r, 1), :] = jnp.transpose(lse)[0:1, :]
                stat_v[1, pl.ds(r, 1), :] = jnp.transpose(tgt)[0:1, :]
            return c
        lax.fori_loop(0, TOK // 512, finish, 0)
        pltpu.make_async_copy(m_s, lse_b, wide_sem.at[0]).start()
        pltpu.make_async_copy(info_v, info_all.at[tp], small_sem.at[0]).wait()
        for h in range(2):
            z_copy(last, h).wait()
        half = e_all.at[pl.ds(0, ROWS // 2)]
        pltpu.make_async_copy(half, half, xs_send).wait()
        pltpu.make_async_copy(half, half, ys_send).wait()
        full = e_all.at[pl.ds(0, ROWS)]
        pltpu.make_async_copy(full, full, ds_send).wait()
        pltpu.make_async_copy(full, full, pe_send).wait()
        own = pltpu.make_async_copy(stat_v, stat_all.at[tp], small_sem.at[1])
        own.start()
        for p, dev in group:
            remote(stat_v, stat_all.at[tp], sm_send, stat_recv.at[p], dev).start()

        def start_xt(j, c):
            xt_copy(j).start()
            return c
        lax.fori_loop(1, XCHS, start_xt, 0)
        xp_copy.start()
        own.wait()
        for i, (src, dst) in enumerate(((m_s, lse_b), (mr_v.at[0], mean_b), (mr_v.at[1], rstd_b))):
            pltpu.make_async_copy(src, dst, wide_sem.at[i]).wait()
    bf16, f32 = jnp.bfloat16, jnp.float32
    wide = pltpu.VMEM((TOK, 128), f32)
    pl.run_scoped(forward, pltpu.VMEM((TOK, DIM), bf16), pltpu.VMEM((2, LN_ROWS, DIM), bf16), pltpu.VMEM((2, TILE, DIM), bf16),
                  pltpu.VMEM((HB, TILE), f32), pltpu.VMEM((HB, TILE), f32), pltpu.VMEM((TOK, 128), jnp.int32), wide, wide, wide,
                  pltpu.VMEM((2, TOK, 128), f32), pltpu.VMEM((2, 8, DIM), f32))

    def dzt_copy(k):
        rows = pl.ds(pl.multiple_of(lax.rem(k, 4) * KT, KT), KT)
        return remote(dzt_out.at[rows], dzt_part.at[rows], dz_send, dz_recv.at[lax.rem(k, 4)], part)

    def token_count():
        return jnp.sum(infos[:, 1].astype(f32))

    def backward(acc):
        def d_phase(zt, et, dz, dzt, lse_v, scale_v, tcol_v):
            lse_load = pltpu.make_async_copy(lse_b, lse_v, wide_sem.at[0])
            lse_load.start()
            for p, dev in group:
                remote(info, info_all.at[tp], sm_send, info_recv.at[p], dev).wait_recv()
            info_load = pltpu.make_async_copy(info_all, infos, small_sem.at[0])
            info_load.start()

            def z_load(k):
                slot = lax.rem(k, 2)
                return pltpu.make_async_copy(z_out.at[:, pl.ds(pl.multiple_of(k * KT, KT), KT)], zt.at[slot], z_sem.at[slot])

            def e_load(k):
                slot = lax.rem(k, 2)
                return pltpu.make_async_copy(e_all.at[pl.ds(pl.multiple_of(k * KT, KT), KT)], et.at[slot], e_sem.at[slot])

            def dzt_store(k, ref):
                return pltpu.make_async_copy(dzt, ref.at[pl.ds(pl.multiple_of(lax.rem(k, 4) * KT, KT), KT)], dzo_sem)
            z_load(0).start()
            e_load(0).start()
            acc[...] = jnp.zeros(acc.shape, jnp.float32)
            info_load.wait()
            lse_load.wait()
            count = jnp.broadcast_to(token_count(), (1, 128))
            for r in range(GROUPS):
                rows = slice(r * 128, (r + 1) * 128)
                spread(info_v[1, r:r + 1, :].astype(f32) / count, rows, scale_v)
                spread(tcol[r:r + 1, :], rows, tcol_v)

            def step(k, c):
                slot = lax.rem(k, 2)

                @pl.when(k + 1 < VOCAB // KT)
                def _():
                    z_load(k + 1).start()
                    e_load(k + 1).start()
                for at, j in WAIT_STEP.items():
                    @pl.when(k == at)
                    def _(j=j):
                        xt_event(j)

                @pl.when((k >= 1) & (k <= 8))
                def _():
                    dzt_store(0, dzt_own).wait()

                @pl.when((k >= 5) & (k <= 8))
                def _():
                    dzt_copy(k - 1).start()
                z_load(k).wait()

                def block(r, c2):
                    rows = pl.ds(pl.multiple_of(r * 256, 256), 256)
                    lane = lax.broadcasted_iota(jnp.int32, (32, 128), 1)
                    for q in range(8):
                        sub = pl.ds(pl.multiple_of(r * 256 + q * 32, 32), 32)
                        lse = lse_v[sub, :]
                        scale = scale_v[sub, :]
                        diff = tcol_v[sub, :] - k * KT
                        for g in range(KT // 128):
                            hot = (diff == lane + g * 128).astype(jnp.float32)
                            val = (jnp.exp(zt[slot, sub, g * 128:(g + 1) * 128] - lse) - hot) * scale
                            dz[sub, g * 128:(g + 1) * 128] = val.astype(jnp.bfloat16)
                    return c2
                lax.fori_loop(0, TOK // 256, block, 0)

                @pl.when(k < 8)
                def _():
                    def flip(r, c2):
                        rows = pl.ds(pl.multiple_of(r * 256, 256), 256)
                        dzt[:, rows] = jnp.transpose(dz[rows, :])
                        return c2
                    lax.fori_loop(0, TOK // 256, flip, 0)

                @pl.when(k < 4)
                def _():
                    dzt_store(k, dzt_own).start()

                @pl.when((k >= 4) & (k < 8))
                def _():
                    dzt_store(k, dzt_out).start()
                e_load(k).wait()

                def mul(h, c2):
                    rows = pl.ds(pl.multiple_of(h * HB, HB), HB)
                    for n in range(0, DIM, NCOL):
                        acc[rows, n:n + NCOL] += jnp.dot(dz[rows, :], et[slot, :, n:n + NCOL], preferred_element_type=jnp.float32)
                    return c2
                lax.fori_loop(0, HBS, mul, 0)
                return c
            lax.fori_loop(0, VOCAB // KT, step, 0)
        pl.run_scoped(d_phase, pltpu.VMEM((2, TOK, KT), jnp.float32), pltpu.VMEM((2, KT, DIM), jnp.bfloat16),
                      pltpu.VMEM((TOK, KT), jnp.bfloat16), pltpu.VMEM((KT, TOK), jnp.bfloat16),
                      pltpu.VMEM((TOK, 128), jnp.float32), pltpu.VMEM((TOK, 128), jnp.float32), pltpu.VMEM((TOK, 128), jnp.int32))

        def n_phase(hb, ob, mr):
            def h_load(i):
                slot = lax.rem(i, 2)
                return pltpu.make_async_copy(hid.at[pl.ds(pl.multiple_of(i * LN_ROWS, LN_ROWS), LN_ROWS)], hb.at[slot], z_sem.at[slot])

            def o_store(i):
                slot = lax.rem(i, 2)
                return pltpu.make_async_copy(ob.at[slot], dhid.at[pl.ds(pl.multiple_of(i * LN_ROWS, LN_ROWS), LN_ROWS)], e_sem.at[slot])
            mr_loads = [pltpu.make_async_copy(src, mr.at[i], wide_sem.at[i]) for i, src in enumerate((mean_b, rstd_b))]
            for cp in mr_loads:
                cp.start()
            h_load(0).start()
            gb_v[...] = jnp.zeros(gb_v.shape, jnp.float32)
            g8[...] = jnp.broadcast_to(gain[...], (8, DIM))
            for cp in mr_loads:
                cp.wait()

            def tile(i, c):
                slot = lax.rem(i, 2)

                @pl.when(i + 1 < TOK // LN_ROWS)
                def _():
                    h_load(i + 1).start()

                @pl.when(i >= 2)
                def _():
                    o_store(i - 2).wait()
                h_load(i).wait()

                def rows_body(r, c2):
                    units = range(NB_UNROLL)
                    base = r * 16 * NB_UNROLL
                    low = [pl.ds(pl.multiple_of(base + u * 16, 16), 16) for u in units]
                    row = [pl.ds(pl.multiple_of(i * LN_ROWS + base + u * 16, 16), 16) for u in units]
                    zero = jnp.zeros((16, 128), jnp.float32)
                    sum1, sum3 = [zero] * NB_UNROLL, [zero] * NB_UNROLL

                    def load(u, cols):
                        dx = acc[row[u], cols]
                        xhat = (hb[slot, low[u], cols].astype(jnp.float32) - mr[0, row[u], :]) * mr[1, row[u], :]
                        return dx, xhat, dx * jnp.concatenate([g8[:, cols]] * 2, axis=0)
                    for k in range(DIM // 128):
                        cols = slice(k * 128, (k + 1) * 128)
                        d_gain, d_bias = gb_v[0, :, cols], gb_v[1, :, cols]
                        for u in units:
                            dx, xhat, gx = load(u, cols)
                            sum1[u] = sum1[u] + gx
                            sum3[u] = sum3[u] + gx * xhat
                            dgx = dx * xhat
                            d_gain = d_gain + (dgx[0:8] + dgx[8:16])
                            d_bias = d_bias + (dx[0:8] + dx[8:16])
                        gb_v[0, :, cols] = d_gain
                        gb_v[1, :, cols] = d_bias
                    c1 = [jnp.broadcast_to(jnp.sum(v, axis=-1, keepdims=True) * (1.0 / DIM), (16, 128)) for v in sum1]
                    c3 = [jnp.broadcast_to(jnp.sum(v, axis=-1, keepdims=True) * (1.0 / DIM), (16, 128)) for v in sum3]
                    for u in units:
                        for k in range(DIM // 128):
                            cols = slice(k * 128, (k + 1) * 128)
                            _, xhat, gx = load(u, cols)
                            ob[slot, low[u], cols] = (mr[1, row[u], :] * (gx - c1[u] - xhat * c3[u])).astype(jnp.bfloat16)
                            acc[row[u], cols] = zero
                    return c2
                lax.fori_loop(0, LN_ROWS // (16 * NB_UNROLL), rows_body, 0)
                o_store(i).start()
                return c
            lax.fori_loop(0, TOK // LN_ROWS, tile, 0)
            for i in range(2):
                o_store(TOK // LN_ROWS - 2 + i).wait()
            gs_v[0:1, :] = jnp.sum(gb_v[0], axis=0, keepdims=True)
            gs_v[1:2, :] = jnp.sum(gb_v[1], axis=0, keepdims=True)
        pl.run_scoped(n_phase, pltpu.VMEM((2, LN_ROWS, DIM), jnp.bfloat16), pltpu.VMEM((2, LN_ROWS, DIM), jnp.bfloat16),
                      pltpu.VMEM((2, TOK, 128), jnp.float32))
        own = pltpu.make_async_copy(gs_v, gsum_all.at[tp], g_sem)

        def e_phase(eo, xt, dzb, zs):
            eo_load = pltpu.make_async_copy(emb, eo, big_sem)

            def x_load(ref, row, slot):
                return pltpu.make_async_copy(ref.at[pl.ds(pl.multiple_of(row, KT), KT)], xt.at[slot], z_sem.at[slot])

            def dz_load(ref, col, slot):
                return pltpu.make_async_copy(ref.at[:, pl.ds(pl.multiple_of(col, KT), KT)], dzb.at[slot], e_sem.at[slot])

            def start_local(i):
                slot = lax.rem(i, 2)

                @pl.when(i < 4)
                def _():
                    x_load(x_out, i * KT, slot).start()
                    dz_load(dzt_own, i * KT, slot).start()

                @pl.when(i >= 4)
                def _():
                    x_load(x_part, (i - 4) * KT, slot).start()
                    dz_load(dzt_part, (i - 4) * KT, slot).start()

            def add(slot):
                def mul(h, c2):
                    rows = pl.ds(pl.multiple_of(h * HB, HB), HB)
                    for n in range(0, DIM, NCOL):
                        acc[rows, n:n + NCOL] += jnp.dot(dzb[slot, rows, :], xt[slot, :, n:n + NCOL], preferred_element_type=jnp.float32)
                    return c2
                lax.fori_loop(0, HBS, mul, 0)

            start_local(0)

            def rem_load(r):
                slot = lax.rem(r, 2)
                return [pltpu.make_async_copy(xrows(ref, r), xt.at[slot, pl.ds(i * XCH, XCH)], z_sem.at[slot])
                        for i, ref in enumerate((x_xp, x_xq))]

            def local(i, c):
                slot = lax.rem(i, 2)

                @pl.when(i == 0)
                def _():
                    eo_load.start()

                @pl.when(i == 2)
                def _():
                    xp_copy.wait_recv()

                    def wait_dz(q, c2):
                        dzt_copy(q).wait_recv()
                        return c2
                    lax.fori_loop(0, 4, wait_dz, 0)

                @pl.when(i == 1)
                def _():
                    own.start()
                    for p, dev in group:
                        remote(gs_v, gsum_all.at[tp], g_send, g_recv.at[p], dev).start()

                @pl.when(i == 1)
                def _():
                    xt_event(4)

                @pl.when(i == 6)
                def _():
                    xt_event(5)

                @pl.when(i < 7)
                def _():
                    start_local(i + 1)

                @pl.when(i == 7)
                def _():
                    xd_copy(0).wait_recv()
                    for cp in rem_load(0):
                        cp.start()
                x_load(x_out, 0, slot).wait()
                dz_load(dzt_own, 0, slot).wait()
                add(slot)
                return c
            lax.fori_loop(0, 8, local, 0)
            eo_load.wait()
            for p, dev in group:
                remote(stat_v, stat_all.at[tp], sm_send, stat_recv.at[p], dev).wait_recv()
            stat_load = pltpu.make_async_copy(stat_all, stats, small_sem.at[1])
            stat_load.start()
            stat_load.wait()
            count = jnp.broadcast_to(token_count(), (1, 128))

            def far(r, c):
                slot = lax.rem(r, 2)

                @pl.when(r == 2)
                def _():
                    xt_event(6)

                @pl.when(r == 6)
                def _():
                    xt_event(7)

                @pl.when(r + 1 < XCHS)
                def _():
                    xd_copy(r + 1).wait_recv()
                    for cp in rem_load(r + 1):
                        cp.start()
                x_load(x_out, 0, slot).wait()

                @pl.when(r == XCHS - DEFER)
                def _():
                    pltpu.make_async_copy(acc, de_part, big_sem).start()

                @pl.when(r > XCHS - DEFER)
                def _():
                    dz_out(0, 0, slot).wait()
                    dz_out(0, 1, slot).wait()

                far_rows = []
                for g in range(4):
                    who = xp_rank if g < 2 else xq_rank
                    at = pl.ds(2 * r + g % 2, 1)
                    far_rows.append((stats[who, 0, at, :], infos[who, 1, at, :].astype(f32) / count, infos[who, 0, at, :] - tp * ROWS))

                def logits(h, c2):
                    for k in range(0, DIM, KCOL):
                        prod = lax.dot_general(eo[pl.ds(pl.multiple_of(h * ZB, ZB), ZB), k:k + KCOL], xt[slot, :, k:k + KCOL], NT, preferred_element_type=jnp.float32)
                        zs[...] = prod if k == 0 else zs[...] + prod
                    for q in range(ZB // 32):
                        row = h * ZB + q * 32
                        line = lax.broadcasted_iota(jnp.int32, (32, 128), 0)
                        for g, (lse, scale, trel) in enumerate(far_rows):
                            cols = slice(g * 128, (g + 1) * 128)
                            hot = ((trel - row) == line).astype(f32)
                            val = (jnp.exp(zs[q * 32:(q + 1) * 32, cols] - lse) - hot) * scale
                            dzb[0, pl.ds(pl.multiple_of(row, 32), 32), cols] = val.astype(bf16)
                    return c2
                lax.fori_loop(0, ROWS // ZB, logits, 0)

                @pl.when(r < XCHS - DEFER)
                def _():
                    def mul(h, c2):
                        rows = pl.ds(pl.multiple_of(h * HB, HB), HB)
                        for n in range(0, DIM, NCOL):
                            acc[rows, n:n + NCOL] += jnp.dot(dzb[0, rows, :], xt[slot, :, n:n + NCOL], preferred_element_type=jnp.float32)
                        return c2
                    lax.fori_loop(0, HBS, mul, 0)

                @pl.when(r >= XCHS - DEFER)
                def _():
                    for i in range(2):
                        dz_out(r - (XCHS - DEFER), i, 0).start()
                return c

            def dz_out(q, i, slot):
                return pltpu.make_async_copy(
                    dzb.at[0, :, pl.ds(i * XCH, XCH)], dzt_last.at[i, :, pl.ds(pl.multiple_of(q * XCH, XCH), XCH)], dzo_sem)
            lax.fori_loop(0, XCHS, far, 0)
            dz_out(0, 0, 0).wait()
            dz_out(0, 1, 0).wait()
            pltpu.make_async_copy(acc, de_part, big_sem).wait()
        pl.run_scoped(e_phase, pltpu.VMEM((ROWS, DIM), jnp.bfloat16), pltpu.VMEM((2, KT, DIM), jnp.bfloat16),
                      pltpu.VMEM((2, ROWS, KT), jnp.bfloat16), pltpu.VMEM((ZB, KT), jnp.float32))

        own.wait()
    pl.run_scoped(backward, pltpu.VMEM((TOK, DIM), f32))

    pltpu.make_async_copy(x_out, x_out, xt_send).wait()
    pltpu.make_async_copy(x_out, x_out, xd_send).wait()
    xp_copy.wait_send()
    pltpu.make_async_copy(dzt_out, dzt_out, dz_send).wait()
    for p, dev in group:
        remote(info, info_all.at[tp], sm_send, info_recv.at[p], dev).wait_send()
        remote(stat_v, stat_all.at[tp], sm_send, stat_recv.at[p], dev).wait_send()
        remote(gs_v, gsum_all.at[tp], g_send, g_recv.at[p], dev).wait()


def run_step(hidden, gain, bias, embed, tcol, info):
    any_spec = pl.BlockSpec(memory_space=pl.ANY)
    vmem_spec = pl.BlockSpec(memory_space=pltpu.VMEM)
    f32, bf16, i32 = jnp.float32, jnp.bfloat16, jnp.int32
    dma = pltpu.SemaphoreType.DMA
    small = (4, 2, GROUPS, 128)
    wide = ((TOK, 128), f32)
    mat, square = ((TOK, DIM), bf16), ((ROWS, TOK), bf16)
    shapes = [((VOCAB, DIM), bf16), mat, ((TOK, VOCAB), f32), (small, f32), (small, i32), wide, wide, wide,
              mat, mat, mat, mat, square, square, square, ((2, ROWS, DEFER * XCH), bf16), ((ROWS, DIM), f32), ((4, 2, DIM), f32)]
    return pl.pallas_call(
        step_kernel,
        name="step",
        out_shape=[jax.ShapeDtypeStruct(s, d) for s, d in shapes],
        in_specs=[any_spec, vmem_spec, vmem_spec, any_spec, vmem_spec, any_spec],
        out_specs=[any_spec] * len(shapes),
        scratch_shapes=[
            pltpu.VMEM((2, GROUPS, 128), i32), pltpu.VMEM((2, GROUPS, 128), f32), pltpu.VMEM(small, f32), pltpu.VMEM(small, i32),
            pltpu.VMEM((2, 8, DIM), f32), pltpu.VMEM((2, DIM), f32), pltpu.VMEM((8, DIM), f32),
            dma((2,)), dma, dma((2,)), dma((2,)), dma((2,)), dma((2,)), dma((3,)), dma, dma, dma,
            dma, dma, dma, dma, dma, dma, dma, dma, dma, dma,
            dma((CHUNKS,)), dma((CHUNKS,)), dma((TILES // 2,)), dma((4,)), dma((4,)), dma((4,)),
            dma((XCHS,)), dma((XCHS,)), dma, dma((4,)), dma((4,)),
        ],
        compiler_params=pltpu.CompilerParams(collective_id=0, has_side_effects=True, vmem_limit_bytes=67043328),
        cost_estimate=pl.CostEstimate(flops=12 * TOK * VOCAB * DIM, bytes_accessed=700 * 2 ** 20, transcendentals=3 * TOK * VOCAB),
    )(hidden, gain, bias, embed, tcol, info)


def finish_kernel(*refs):
    nb = DEFER * XCH // KT
    de_in, dz0, dz1 = refs[:3]
    xs = refs[3:3 + 2 * nb]
    dh_in, stat_all, info_all, gsum_all, de_out, dh_out, loss, mean, sums = refs[3 + 2 * nb:]
    prod = de_in[...]
    for b in range(nb):
        prod = prod + jnp.dot(dz0[0, :, b * KT:(b + 1) * KT], xs[b][...], preferred_element_type=jnp.float32)
        prod = prod + jnp.dot(dz1[0, :, b * KT:(b + 1) * KT], xs[nb + b][...], preferred_element_type=jnp.float32)
    de_out[...] = prod
    dh_out[...] = dh_in[...]

    @pl.when(pl.program_id(0) == 0)
    def _():
        weights = info_all[:, 1].astype(jnp.float32)
        all_loss = (stat_all[:, 0] - stat_all[:, 1]) * weights
        tp = lax.axis_index('tp')
        loss[...] = (stat_all[tp, 0] - stat_all[tp, 1]) * info_all[tp, 1].astype(jnp.float32)
        mean[...] = jnp.broadcast_to(jnp.sum(all_loss), (1, 128)) / jnp.broadcast_to(jnp.sum(weights), (1, 128))
        sums[...] = ((gsum_all[0] + gsum_all[1]) + gsum_all[2]) + gsum_all[3]


def finish(de_part, dzt_last, x_xp, x_xq, dhid, stat_all, info_all, gsum_all):
    cols = 512
    steps = DIM // cols
    depth = DEFER * XCH
    rows = TOK // steps
    first = (TOK - depth) // KT
    once = pl.Buffered(1)
    x_specs = [pl.BlockSpec((KT, cols), lambda i, b=b: (b, i)) for b in range(first, TOK // KT)]

    def whole(shape):
        return pl.BlockSpec(shape, lambda i: (0,) * len(shape))
    nb = len(x_specs)
    outs = [((ROWS, DIM), jnp.float32), ((TOK, DIM), jnp.bfloat16), ((GROUPS, 128), jnp.float32), ((1, 128), jnp.float32), ((2, DIM), jnp.float32)]
    return pl.pallas_call(
        finish_kernel,
        name="finish",
        grid=(steps,),
        out_shape=[jax.ShapeDtypeStruct(s, d) for s, d in outs],
        in_specs=[
            pl.BlockSpec((ROWS, cols), lambda i: (0, i)),
            pl.BlockSpec((1, ROWS, depth), lambda i: (0, 0, 0), pipeline_mode=once),
            pl.BlockSpec((1, ROWS, depth), lambda i: (1, 0, 0), pipeline_mode=once),
            *x_specs, *x_specs,
            pl.BlockSpec((rows, DIM), lambda i: (i, 0)),
            whole(stat_all.shape), whole(info_all.shape), whole(gsum_all.shape),
        ],
        out_specs=[pl.BlockSpec((ROWS, cols), lambda i: (0, i)), pl.BlockSpec((rows, DIM), lambda i: (i, 0)),
                   whole((GROUPS, 128)), whole((1, 128)), whole((2, DIM))],
        compiler_params=pltpu.CompilerParams(vmem_limit_bytes=60 * 1024 * 1024),
        cost_estimate=pl.CostEstimate(flops=4 * ROWS * DIM * depth, bytes_accessed=120 * 2 ** 20, transcendentals=0),
    )(de_part, dzt_last, dzt_last, *[x_xp] * nb, *[x_xq] * nb, dhid, stat_all, info_all, gsum_all)


def solution(mesh):
    def body(hidden, ln_gain, ln_bias, embed, targets, loss_mask):
        dp, rank = lax.axis_index('dp'), lax.axis_index('tp')
        info = jnp.stack([targets, loss_mask]).reshape(2, GROUPS, 128)
        shard = targets // ROWS
        block = jnp.bitwise_xor(shard, rank)
        row = targets % ROWS
        half = row // (ROWS // 2)
        sub = row % (ROWS // 2)
        piece = (block - 2) * 2 + jnp.bitwise_xor(half, dp)
        far = 2 * ROWS + (sub // 128) * TILE + piece * 128 + sub % 128
        tcol = jnp.where(block < 2, block * ROWS + row, far).reshape(GROUPS, 128)
        outs = run_step(hidden, ln_gain.reshape(1, DIM), ln_bias.reshape(1, DIM), embed, tcol, info)
        stat_all, info_all, dhid, x_xp, x_xq, dzt_last, de_part, gsum_all = (outs[i] for i in (3, 4, 8, 10, 11, 15, 16, 17))
        d_embed, d_hidden, loss, mean, sums = finish(de_part, dzt_last, x_xp, x_xq, dhid, stat_all, info_all, gsum_all)
        return loss.reshape(TOK), mean[0, :1], d_hidden, d_embed, sums[0], sums[1]

    token_rows = P(('dp', 'tp'))
    token_mat = P(('dp', 'tp'), None)
    return jax.shard_map(body, mesh=mesh, in_specs=(token_mat, P(), P(), P('tp', None), token_rows, token_rows), out_specs=(token_rows, P('dp'), token_mat, token_mat, P('dp'), P('dp')), check_vma=False)
```

time: 1740 us -> 694 us (0.40)
  waiting for transfers between devices: 1100 us -> 0 us
  Pallas kernels: 0 us -> 689 us
  matrix products: 475 us -> 0 us
  other arithmetic: 101 us -> 2.65 us
  blocking collectives: 45.4 us -> 0 us
    unnamed x4 -> x0, waiting for transfers between devices: 702 us -> none
    pallas_call x0 -> x2, Pallas kernels: none -> 689 us  [the longest x1 623 us: run_step(): pl.pallas_call(step_kernel, name='step', out_shape=[jax.ShapeDtypeStruct(...]
    dot_general x3 -> x0, matrix products: 475 us -> none  [the longest x1 166 us: body(): jnp.einsum('sv,sd->vd', d_logits, gathered, preferred_element_type=jnp.fl...]
    all_gather x1 -> x0, waiting for transfers between devices: 382 us -> none  [body(): gathered = lax.all_gather(normed, 'tp', tiled=True)]
    reduce_sum x6 -> x0, other arithmetic: 63.2 us -> none  [the longest x1 21.5 us: body(): local_sum = jnp.sum(jnp.exp(logits - local_max[:, None]), axis=-1)]
    convert_element_type x2 -> x0, other arithmetic: 36.7 us -> none  [the longest x1 25.7 us: norm_backward(): (inv_std * (value_a6 - centre_term - x_hat * proj_term)).astype(jnp.bfloa...]
    all_gather x2 -> x0, blocking collectives: 18.4 us -> none  [the longest x1 9.98 us: body(): all_targets = lax.all_gather(targets, 'tp', tiled=True)]
  transfers between devices with their start and end apart: 3 -> 0, of which waited for: 3 -> 0; matrix products, arithmetic and copies ran while one was open for 10% -> 0% of each run, Pallas kernels for 0% -> 0%
where the time goes in v1:
time: 694 us
  Pallas kernels  689 us (99%)
    pallas_call x1, Pallas kernels, run_step(): pl.pallas_call(step_kernel, name='step', out_shape=[jax.ShapeDtypeStruct(...  623 us
    pallas_call x1, Pallas kernels, finish(): pl.pallas_call(finish_kernel, name='finish', grid=(steps,), out_shape=[ja...  66.1 us

profile of v1, /device:TPU:0, one launch (start us, length us, event | category | flops | bytes accessed | tf_op | source)
XLA Modules:
  0.0 693.7 jit_solution(1283809649982781301)
XLA Ops:
  0.6 1.3 fusion.6.tcol
  2.0 1.3 pad_add_fusion.info
  3.3 622.8 %step.1 = (bf16[8192,4096]{1,0:T(8,128)(2,1)}, bf16[2048,4096]{1,0:T(8,128)(2,1)}, f32[2048,8192]{1,0:T(8,128)}, f32[4,2,16,128]{3,2,1,0:T(8,128)}, s32[4,2,16,1...) custom-call(bf16[2048,4096]{1,0:T(8,128)(2,1)} %hid.1, ...), custom_call_target="tpu_custom_call" | custom-call | flops 824633720832 | bytes 734003200 | tf_op jit(solution)/shard_map/step/pallas_call | solution.py:723
  626.1 66.1 %finish.1 = (f32[2048,4096]{1,0:T(8,128)}, bf16[2048,4096]{1,0:T(8,128)(2,1)}, f32[16,128]{1,0:T(8,128)}, f32[1,128]{1,0:T(1,128)}, f32[2,4096]{1,0:T(2,128)}) custom-call(f32[2048,4096]{1,0:T(8,128)} %get-tuple-element.19.refs_0_, bf16[2,2048,1536]{2,1,0:T(8,128)(2,1)} %get-tuple-element.20.refs_1_.refs_2_, ...), custom_call_target="tpu_custom_call" | custom-call | flops 51539607552 | bytes 125829120 | tf_op jit(solution)/shard_map/finish/pallas_call | solution.py:777
  692.2 1.5 fusion.17

commit v2 on v1

--- a/solution.py
+++ b/solution.py
@@ -21,13 +21,14 @@
 CHUNK = 64
 CHUNKS = ROWS // 2 // CHUNK
 LN_ROWS = 256
-STAT_ROWS = 16
+STAT_ROWS = 32
+PIECE = 32
 LN_UNROLL = 4
 XCH = 256
 XCHS = TOK // XCH
 KT = 512
-DEFER = 6
-WAIT_STEP = {2: 0, 6: 1, 10: 2, 15: 3}
+DEFER = 4
+WAIT_STEP = {2: 0, 7: 1, 13: 2}
 ZB = 512
 NCOL = 512
 KCOL = 1024
@@ -367,7 +368,7 @@
         return jnp.sum(infos[:, 1].astype(f32))
 
     def backward(acc):
-        def d_phase(zt, et, dz, dzt, lse_v, scale_v, tcol_v):
+        def d_phase(zt, et, da, db, dzt, lse_v, scale_v, tcol_v):
             lse_load = pltpu.make_async_copy(lse_b, lse_v, wide_sem.at[0])
             lse_load.start()
             for p, dev in group:
@@ -384,7 +385,8 @@
                 return pltpu.make_async_copy(e_all.at[pl.ds(pl.multiple_of(k * KT, KT), KT)], et.at[slot], e_sem.at[slot])
 
             def dzt_store(k, ref):
-                return pltpu.make_async_copy(dzt, ref.at[pl.ds(pl.multiple_of(lax.rem(k, 4) * KT, KT), KT)], dzo_sem)
+                slot = lax.rem(k, 2)
+                return pltpu.make_async_copy(dzt.at[slot], ref.at[pl.ds(pl.multiple_of(lax.rem(k, 4) * KT, KT), KT)], eo_sem.at[slot])
             z_load(0).start()
             e_load(0).start()
             acc[...] = jnp.zeros(acc.shape, jnp.float32)
@@ -396,9 +398,46 @@
                 spread(info_v[1, r:r + 1, :].astype(f32) / count, rows, scale_v)
                 spread(tcol[r:r + 1, :], rows, tcol_v)
 
+            lane = lax.broadcasted_iota(jnp.int32, (PIECE, 128), 1)
+
+            def piece(dst, rows, low, k, tie):
+                slot = lax.rem(k, 2)
+                lse = lse_v[rows, :]
+                if tie is not None:
+                    floor = 0.0 - jnp.maximum(0.0 - tie, -LOWEST)
+                    lse = jnp.maximum(lse, jnp.concatenate([floor] * (PIECE // 8), axis=0))
+                scale = scale_v[rows, :]
+                diff = tcol_v[rows, :] - k * KT
+                for g in range(KT // 128):
+                    cols = slice(g * 128, (g + 1) * 128)
+                    hot = (diff == lane + g * 128).astype(f32)
+                    val = (jnp.exp(zt[slot, rows, cols] - lse) - hot) * scale
+                    dst[low, cols] = val.astype(bf16)
+
+            def half_step(k, src, dst, base, dst_base, dst_k):
+                slot = lax.rem(k, 2)
+                per = HB // (DIM // NCOL)
+                for n in range(DIM // NCOL):
+                    cols = slice(n * NCOL, (n + 1) * NCOL)
+                    prod = jnp.dot(src[...], et[slot, :, cols], preferred_element_type=f32)
+                    acc[base:base + HB, cols] += prod
+                    for q in range(0, per, PIECE):
+                        at = q * HB // per
+                        low = n * per + q
+                        piece(dst, slice(dst_base + low, dst_base + low + PIECE), slice(low, low + PIECE), dst_k, prod[at:at + 8, 0:128])
+                    if n * per % 256 == 0:
+                        low = n * per
+                        dzt[slot, :, base + low:base + low + 256] = jnp.transpose(src[low:low + 256, :])
+
+            z_load(0).wait()
+
+            def first(i, c):
+                rows = pl.ds(pl.multiple_of(i * PIECE, PIECE), PIECE)
+                piece(da, rows, rows, 0, None)
+                return c
+            lax.fori_loop(0, HB // PIECE, first, 0)
+
             def step(k, c):
-                slot = lax.rem(k, 2)
-
                 @pl.when(k + 1 < VOCAB // KT)
                 def _():
                     z_load(k + 1).start()
@@ -408,37 +447,20 @@
                     def _(j=j):
                         xt_event(j)
 
-                @pl.when((k >= 1) & (k <= 8))
-                def _():
-                    dzt_store(0, dzt_own).wait()
-
-                @pl.when((k >= 5) & (k <= 8))
-                def _():
-                    dzt_copy(k - 1).start()
-                z_load(k).wait()
-
-                def block(r, c2):
-                    rows = pl.ds(pl.multiple_of(r * 256, 256), 256)
-                    lane = lax.broadcasted_iota(jnp.int32, (32, 128), 1)
-                    for q in range(8):
-                        sub = pl.ds(pl.multiple_of(r * 256 + q * 32, 32), 32)
-                        lse = lse_v[sub, :]
-                        scale = scale_v[sub, :]
-                        diff = tcol_v[sub, :] - k * KT
-                        for g in range(KT // 128):
-                            hot = (diff == lane + g * 128).astype(jnp.float32)
-                            val = (jnp.exp(zt[slot, sub, g * 128:(g + 1) * 128] - lse) - hot) * scale
-                            dz[sub, g * 128:(g + 1) * 128] = val.astype(jnp.bfloat16)
-                    return c2
-                lax.fori_loop(0, TOK // 256, block, 0)
-
-                @pl.when(k < 8)
-                def _():
-                    def flip(r, c2):
-                        rows = pl.ds(pl.multiple_of(r * 256, 256), 256)
-                        dzt[:, rows] = jnp.transpose(dz[rows, :])
-                        return c2
-                    lax.fori_loop(0, TOK // 256, flip, 0)
+                @pl.when((k >= 2) & (k < 10))
+                def _():
+                    dzt_store(k, dzt_own).wait()
+
+                @pl.when((k >= 6) & (k < 10))
+                def _():
+                    dzt_copy(k - 2).start()
+                e_load(k).wait()
+                half_step(k, da, db, 0, HB, k)
+
+                @pl.when(k + 1 < VOCAB // KT)
+                def _():
+                    z_load(k + 1).wait()
+                half_step(k, db, da, HB, 0, k + 1)
 
                 @pl.when(k < 4)
                 def _():
@@ -447,19 +469,11 @@
                 @pl.when((k >= 4) & (k < 8))
                 def _():
                     dzt_store(k, dzt_out).start()
-                e_load(k).wait()
-
-                def mul(h, c2):
-                    rows = pl.ds(pl.multiple_of(h * HB, HB), HB)
-                    for n in range(0, DIM, NCOL):
-                        acc[rows, n:n + NCOL] += jnp.dot(dz[rows, :], et[slot, :, n:n + NCOL], preferred_element_type=jnp.float32)
-                    return c2
-                lax.fori_loop(0, HBS, mul, 0)
                 return c
             lax.fori_loop(0, VOCAB // KT, step, 0)
-        pl.run_scoped(d_phase, pltpu.VMEM((2, TOK, KT), jnp.float32), pltpu.VMEM((2, KT, DIM), jnp.bfloat16),
-                      pltpu.VMEM((TOK, KT), jnp.bfloat16), pltpu.VMEM((KT, TOK), jnp.bfloat16),
-                      pltpu.VMEM((TOK, 128), jnp.float32), pltpu.VMEM((TOK, 128), jnp.float32), pltpu.VMEM((TOK, 128), jnp.int32))
+        half = pltpu.VMEM((HB, KT), bf16)
+        pl.run_scoped(d_phase, pltpu.VMEM((2, TOK, KT), f32), pltpu.VMEM((2, KT, DIM), bf16), half, half, pltpu.VMEM((2, KT, TOK), bf16),
+                      pltpu.VMEM((TOK, 128), f32), pltpu.VMEM((TOK, 128), f32), pltpu.VMEM((TOK, 128), jnp.int32))
 
         def n_phase(hb, ob, mr):
             def h_load(i):
@@ -534,6 +548,7 @@
         pl.run_scoped(n_phase, pltpu.VMEM((2, LN_ROWS, DIM), jnp.bfloat16), pltpu.VMEM((2, LN_ROWS, DIM), jnp.bfloat16),
                       pltpu.VMEM((2, TOK, 128), jnp.float32))
         own = pltpu.make_async_copy(gs_v, gsum_all.at[tp], g_sem)
+        xt_event(3)
 
         def e_phase(eo, xt, dzb, zs):
             eo_load = pltpu.make_async_copy(emb, eo, big_sem)
@@ -594,13 +609,9 @@
                     for p, dev in group:
                         remote(gs_v, gsum_all.at[tp], g_send, g_recv.at[p], dev).start()
 
-                @pl.when(i == 1)
+                @pl.when(i == 4)
                 def _():
                     xt_event(4)
-
-                @pl.when(i == 6)
-                def _():
-                    xt_event(5)
 
                 @pl.when(i < 7)
                 def _():
@@ -627,7 +638,11 @@
             def far(r, c):
                 slot = lax.rem(r, 2)
 
-                @pl.when(r == 2)
+                @pl.when(r == 1)
+                def _():
+                    xt_event(5)
+
+                @pl.when(r == 3)
                 def _():
                     xt_event(6)
 
@@ -646,7 +661,7 @@
                 def _():
                     pltpu.make_async_copy(acc, de_part, big_sem).start()
 
-                @pl.when(r > XCHS - DEFER)
+                @pl.when(r > XCHS - DEFER + 1)
                 def _():
                     dz_out(0, 0, slot).wait()
                     dz_out(0, 1, slot).wait()
@@ -668,7 +683,7 @@
                             cols = slice(g * 128, (g + 1) * 128)
                             hot = ((trel - row) == line).astype(f32)
                             val = (jnp.exp(zs[q * 32:(q + 1) * 32, cols] - lse) - hot) * scale
-                            dzb[0, pl.ds(pl.multiple_of(row, 32), 32), cols] = val.astype(bf16)
+                            dzb[slot, pl.ds(pl.multiple_of(row, 32), 32), cols] = val.astype(bf16)
                     return c2
                 lax.fori_loop(0, ROWS // ZB, logits, 0)
 
@@ -677,22 +692,23 @@
                     def mul(h, c2):
                         rows = pl.ds(pl.multiple_of(h * HB, HB), HB)
                         for n in range(0, DIM, NCOL):
-                            acc[rows, n:n + NCOL] += jnp.dot(dzb[0, rows, :], xt[slot, :, n:n + NCOL], preferred_element_type=jnp.float32)
+                            acc[rows, n:n + NCOL] += jnp.dot(dzb[slot, rows, :], xt[slot, :, n:n + NCOL], preferred_element_type=jnp.float32)
                         return c2
                     lax.fori_loop(0, HBS, mul, 0)
 
                 @pl.when(r >= XCHS - DEFER)
                 def _():
                     for i in range(2):
-                        dz_out(r - (XCHS - DEFER), i, 0).start()
+                        dz_out(r - (XCHS - DEFER), i, slot).start()
                 return c
 
             def dz_out(q, i, slot):
                 return pltpu.make_async_copy(
-                    dzb.at[0, :, pl.ds(i * XCH, XCH)], dzt_last.at[i, :, pl.ds(pl.multiple_of(q * XCH, XCH), XCH)], dzo_sem)
+                    dzb.at[slot, :, pl.ds(i * XCH, XCH)], dzt_last.at[i, :, pl.ds(pl.multiple_of(q * XCH, XCH), XCH)], dzo_sem.at[slot])
             lax.fori_loop(0, XCHS, far, 0)
-            dz_out(0, 0, 0).wait()
-            dz_out(0, 1, 0).wait()
+            for slot in range(2):
+                dz_out(0, 0, slot).wait()
+                dz_out(0, 1, slot).wait()
             pltpu.make_async_copy(acc, de_part, big_sem).wait()
         pl.run_scoped(e_phase, pltpu.VMEM((ROWS, DIM), jnp.bfloat16), pltpu.VMEM((2, KT, DIM), jnp.bfloat16),
                       pltpu.VMEM((2, ROWS, KT), jnp.bfloat16), pltpu.VMEM((ZB, KT), jnp.float32))
@@ -729,7 +745,7 @@
         scratch_shapes=[
             pltpu.VMEM((2, GROUPS, 128), i32), pltpu.VMEM((2, GROUPS, 128), f32), pltpu.VMEM(small, f32), pltpu.VMEM(small, i32),
             pltpu.VMEM((2, 8, DIM), f32), pltpu.VMEM((2, DIM), f32), pltpu.VMEM((8, DIM), f32),
-            dma((2,)), dma, dma((2,)), dma((2,)), dma((2,)), dma((2,)), dma((3,)), dma, dma, dma,
+            dma((2,)), dma, dma((2,)), dma((2,)), dma((2,)), dma((2,)), dma((3,)), dma((2,)), dma, dma,
             dma, dma, dma, dma, dma, dma, dma, dma, dma, dma,
             dma((CHUNKS,)), dma((CHUNKS,)), dma((TILES // 2,)), dma((4,)), dma((4,)), dma((4,)),
             dma((XCHS,)), dma((XCHS,)), dma, dma((4,)), dma((4,)),

time: 694 us -> 662 us (0.954)
  Pallas kernels: 689 us -> 657 us
    pallas_call x1, Pallas kernels: 623 us -> 607 us  [run_step(): pl.pallas_call(step_kernel, name='step', out_shape=[jax.ShapeDtypeStruct(...]
    pallas_call x1, Pallas kernels: 66.1 us -> 50 us  [finish(): pl.pallas_call(finish_kernel, name='finish', grid=(steps,), out_shape=[ja...]
where the time goes in v2:
time: 662 us; the launch traced here: 661 us
  Pallas kernels  657 us (99%)
    pallas_call x1, Pallas kernels, run_step(): pl.pallas_call(step_kernel, name='step', out_shape=[jax.ShapeDtypeStruct(...  607 us
    pallas_call x1, Pallas kernels, finish(): pl.pallas_call(finish_kernel, name='finish', grid=(steps,), out_shape=[ja...  50 us

profile of v2, /device:TPU:0, one launch (start us, length us, event | category | flops | bytes accessed | tf_op | source)
XLA Modules:
  0.0 661.4 jit_solution(4459765835547658108)
XLA Ops:
  0.6 1.3 fusion.6.tcol
  2.0 1.3 pad_add_fusion.info
  3.3 606.6 %step.1 = (bf16[8192,4096]{1,0:T(8,128)(2,1)}, bf16[2048,4096]{1,0:T(8,128)(2,1)}, f32[2048,8192]{1,0:T(8,128)}, f32[4,2,16,128]{3,2,1,0:T(8,128)}, s32[4,2,16,1...) custom-call(bf16[2048,4096]{1,0:T(8,128)(2,1)} %hid.1, ...), custom_call_target="tpu_custom_call" | custom-call | flops 824633720832 | bytes 734003200 | tf_op jit(solution)/shard_map/step/pallas_call | solution.py:739
  609.9 50.0 %finish.1 = (f32[2048,4096]{1,0:T(8,128)}, bf16[2048,4096]{1,0:T(8,128)(2,1)}, f32[16,128]{1,0:T(8,128)}, f32[1,128]{1,0:T(1,128)}, f32[2,4096]{1,0:T(2,128)}) custom-call(f32[2048,4096]{1,0:T(8,128)} %get-tuple-element.19.refs_0_, bf16[2,2048,1024]{2,1,0:T(8,128)(2,1)} %get-tuple-element.20.refs_1_.refs_2_, ...), custom_call_target="tpu_custom_call" | custom-call | flops 34359738368 | bytes 125829120 | tf_op jit(solution)/shard_map/finish/pallas_call | solution.py:793
  660.0 1.5 fusion.17

commit v3 on v2

--- a/solution.py
+++ b/solution.py
@@ -14,11 +14,14 @@
 ROWS = 2048
 DIM = 4096
 VOCAB = 8192
-TILE = 512
+TILE = 256
 TILES = VOCAB // TILE
 HB = 1024
 HBS = TOK // HB
-CHUNK = 64
+CHUNK = 32
+PIECE_ROWS = 2 * CHUNK
+NEAR = 2 * ROWS // TILE
+PE_ROWS = 512
 CHUNKS = ROWS // 2 // CHUNK
 LN_ROWS = 256
 STAT_ROWS = 32
@@ -28,11 +31,12 @@
 XCHS = TOK // XCH
 KT = 512
 DEFER = 4
-WAIT_STEP = {2: 0, 7: 1, 13: 2}
+WAIT_STEP = {4: 0, 9: 1, 14: 2}
 ZB = 512
 NCOL = 512
 KCOL = 1024
 NB_UNROLL = 8
+NB_ROWS = 128
 GROUPS = TOK // 128
 NT = (((1,), (1,)), ((), ()))
 
@@ -55,13 +59,14 @@
     dst[rows, :] = jnp.transpose(jnp.broadcast_to(row, (128, 128)))
 
 
-def step_kernel(hid, gain, bias, emb, tcol, info,
-                e_all, x_out, z_out, stat_all, info_all, lse_b, mean_b, rstd_b,
+def step_kernel(hid, gain, bias, emb, info,
+                e_all, x_out, z_out, stat_all, info_all,
                 dhid, x_part, x_xp, x_xq, dzt_own, dzt_out, dzt_part, dzt_last, de_part, gsum_all,
                 info_v, stat_v, stats, infos, gb_v, gs_v, g8,
-                h_sem, xo_sem, e_sem, eo_sem, z_sem, small_sem, wide_sem, dzo_sem, big_sem, g_sem,
+                h_sem, xo_sem, e_sem, eo_sem, z_sem, zt_sem, et_sem, small_sem, dzo_sem, big_sem, g_sem,
                 xs_send, ys_send, ds_send, pe_send, sm_send, xt_send, xd_send, xp_send, dz_send, g_send,
                 x_recv, y_recv, d_recv, pe_recv, info_recv, stat_recv, xt_recv, xd_recv, xp_recv, dz_recv, g_recv):
+    bf16, f32 = jnp.bfloat16, jnp.float32
     dp, tp, part, xp, xq, yp = peers()
     core = lax.rem(tp, 2)
     xp_rank = 2 - (tp - core) + core
@@ -86,7 +91,7 @@
         xd_copy(j).start()
     xp_copy = remote(x_out, x_part, xp_send, xp_recv, part)
 
-    def forward(xs, hbuf, ebuf, z0, z1, tc_v, m_s, s_s, t_s, mr_v, gb8):
+    def forward(m_s, scale_v, tc_v, mr_v, zt, et, xs, hbuf, ebuf, z0, z1, s_s, t_s, gb8):
         def tile_row(j):
             return ROWS * 2 + (j // 2) * TILE + lax.rem(j, 2) * CHUNK
 
@@ -95,7 +100,7 @@
             return remote(src, e_all.at[pl.ds(pl.multiple_of(tile_row(j), CHUNK), CHUNK)], xs_send, x_recv.at[j], xp)
 
         def piece(j, p):
-            return e_all.at[pl.ds(pl.multiple_of(tile_row(j) + p * 2 * CHUNK, CHUNK), CHUNK)]
+            return e_all.at[pl.ds(pl.multiple_of(tile_row(j) + p * PIECE_ROWS, CHUNK), CHUNK)]
 
         def y_copy(j):
             return remote(piece(j, 0), piece(j, 1), ys_send, y_recv.at[j], yp)
@@ -104,8 +109,8 @@
             return remote(piece(j, p), piece(j, p + 2), ds_send, d_recv.at[j // 2], part)
 
         def pe_copy(i):
-            return remote(emb.at[pl.ds(pl.multiple_of(i * TILE, TILE), TILE)],
-                          e_all.at[pl.ds(pl.multiple_of(ROWS + i * TILE, TILE), TILE)], pe_send, pe_recv.at[i], part)
+            return remote(emb.at[pl.ds(pl.multiple_of(i * PE_ROWS, PE_ROWS), PE_ROWS)],
+                          e_all.at[pl.ds(pl.multiple_of(ROWS + i * PE_ROWS, PE_ROWS), PE_ROWS)], pe_send, pe_recv.at[i], part)
 
         cp = pltpu.make_async_copy(info, info_v, small_sem.at[0])
         cp.start()
@@ -125,7 +130,7 @@
         def start_pe(i, c):
             pe_copy(i).start()
             return c
-        lax.fori_loop(0, ROWS // TILE, start_pe, 0)
+        lax.fori_loop(0, ROWS // PE_ROWS, start_pe, 0)
 
         def e_load(t):
             slot = lax.rem(t, 2)
@@ -136,6 +141,20 @@
             return pltpu.make_async_copy(emb.at[pl.ds(pl.multiple_of(t * TILE, TILE), TILE)], ebuf.at[slot], e_sem.at[slot])
         e_load_own(0).start()
 
+        def x_event(j):
+            x_copy(j).wait_recv()
+            y_copy(j).start()
+            d_copy(j, 0).start()
+
+        def y_event(j):
+            y_copy(j).wait_recv()
+            d_copy(j, 1).start()
+
+        def p_event(k):
+            rows = e_all.at[pl.ds(pl.multiple_of(2 * ROWS + k * TILE + TILE // 2, TILE // 2), TILE // 2)]
+            pltpu.make_async_copy(rows, rows, d_recv.at[k]).wait()
+            e_load(NEAR + k).start()
+
         cp.wait()
         pltpu.make_async_copy(info_v, info_all.at[tp], small_sem.at[0]).start()
         gb8[0] = jnp.broadcast_to(gain[...], (8, DIM))
@@ -148,6 +167,10 @@
             def _():
                 h_copy(i + 1).start()
             h_copy(i).wait()
+
+            @pl.when(i == 6)
+            def _():
+                x_event(0)
 
             def ln_rows(r, c2):
                 base = r * LN_UNROLL * 16
@@ -186,19 +209,19 @@
             return c
         lax.fori_loop(0, TOK // LN_ROWS, ln_tile, 0)
 
-        for i, dst in enumerate((mean_b, rstd_b)):
-            pltpu.make_async_copy(mr_v.at[i], dst, wide_sem.at[i + 1]).start()
         m_s[...] = jnp.full((TOK, 128), LOWEST, jnp.float32)
         s_s[...] = jnp.zeros((TOK, 128), jnp.float32)
         t_s[...] = jnp.zeros((TOK, 128), jnp.float32)
         for r in range(GROUPS):
-            spread(tcol[r:r + 1, :], slice(r * 128, (r + 1) * 128), tc_v)
+            spread(info_v[2, r:r + 1, :], slice(r * 128, (r + 1) * 128), tc_v)
         z1[...] = jnp.full((HB, TILE), LOWEST, jnp.float32)
 
         zs = (z0, z1)
 
         def product(t, h):
-            zs[h][...] = lax.dot_general(xs[h * HB:(h + 1) * HB, :], ebuf[lax.rem(t, 2)], NT, preferred_element_type=jnp.float32)
+            for r in range(0, HB, 512):
+                zs[h][r:r + 512, :] = lax.dot_general(
+                    xs[h * HB + r:h * HB + r + 512, :], ebuf[lax.rem(t, 2)], NT, preferred_element_type=jnp.float32)
 
         def statistics(t, h):
             z = zs[h]
@@ -207,7 +230,7 @@
                 rows = slice(h * HB + r, h * HB + r + STAT_ROWS)
                 zk = [z[r:r + STAT_ROWS, k * 128:(k + 1) * 128] for k in range(TILE // 128)]
                 old = m_s[rows, :]
-                new = jnp.maximum(jnp.maximum(jnp.maximum(zk[0], zk[1]), jnp.maximum(zk[2], zk[3])), old)
+                new = jnp.maximum(jnp.maximum(zk[0], zk[1]), old)
                 tot = s_s[rows, :] * jnp.exp(old - new)
                 tgt = t_s[rows, :]
                 diff = tc_v[rows, :] - t * TILE
@@ -222,75 +245,66 @@
             return pltpu.make_async_copy(
                 zs[h], z_out.at[pl.ds(h * HB, HB), pl.ds(pl.multiple_of(t * TILE, TILE), TILE)], z_sem.at[h])
 
-        def x_event(j):
-            x_copy(j).wait_recv()
-            y_copy(j).start()
-            d_copy(j, 0).start()
-
-        def y_event(j):
-            y_copy(j).wait_recv()
-            d_copy(j, 1).start()
-
-        def p_event(k):
-            rows = e_all.at[pl.ds(pl.multiple_of(2 * ROWS + k * TILE + TILE // 2, TILE // 2), TILE // 2)]
-            pltpu.make_async_copy(rows, rows, d_recv.at[k]).wait()
-            e_load(8 + k).start()
-
-        half_tiles = TILES // 2
-
         def start_events(t):
             @pl.when(t < TILES - 1)
             def _():
-                x_event(t)
+                x_event(t + 1)
 
             @pl.when(t == TILES - 2)
             def _():
                 xt_copy(0).start()
-                y_event(TILES - 3)
-                p_event(6)
 
             @pl.when(t == TILES - 1)
             def _():
-                y_event(TILES - 2)
                 y_event(TILES - 1)
-                p_event(7)
+                p_event(TILES - 1 - NEAR)
             e_load(t).wait()
 
-            @pl.when(t < 4)
+            @pl.when(t < ROWS // TILE)
             def _():
                 slot = lax.rem(t, 2)
                 pltpu.make_async_copy(ebuf.at[slot], e_all.at[pl.ds(pl.multiple_of(t * TILE, TILE), TILE)], eo_sem.at[slot]).start()
 
         def middle_events(t):
-            @pl.when((t >= 1) & (t < TILES - 2))
-            def _():
-                y_event(t - 1)
-
-            @pl.when((t >= 1) & (t < 5))
+            @pl.when(t < TILES - 1)
+            def _():
+                y_event(t)
+
+            @pl.when((t >= 1) & (t < ROWS // TILE + 1))
             def _():
                 slot = lax.rem(t - 1, 2)
                 pltpu.make_async_copy(ebuf.at[slot], e_all.at[pl.ds(0, TILE)], eo_sem.at[slot]).wait()
 
-            @pl.when(t == 8)
+            @pl.when(t == NEAR)
             def _():
                 pltpu.make_async_copy(xs, x_out, xo_sem).wait()
 
-            @pl.when(t < 3)
+            @pl.when(t < ROWS // TILE - 1)
             def _():
                 e_load_own(t + 1).start()
 
-            @pl.when((t >= 3) & (t < 7))
-            def _():
-                pe_copy(t - 3).wait_recv()
+            @pl.when((t >= ROWS // TILE - 1) & (t < NEAR - 1))
+            def _():
+                @pl.when(lax.rem(t + 1, PE_ROWS // TILE) == 0)
+                def _():
+                    pe_copy((t + 1 - ROWS // TILE) // (PE_ROWS // TILE)).wait_recv()
                 e_load(t + 1).start()
 
-            @pl.when((t >= half_tiles - 1) & (t < TILES - 3))
-            def _():
-                p_event(t - (half_tiles - 1))
-
-            @pl.when(t == TILES - 2)
-            def _():
-                x_event(TILES - 1)
+            @pl.when((t >= NEAR - 1) & (t < TILES - 2))
+            def _():
+                p_event(t - (NEAR - 1))
+
+            @pl.when(t == NEAR + 1)
+            def _():
+                for p, dev in group:
+                    remote(info, info_all.at[tp], sm_send, info_recv.at[p], dev).wait_recv()
+                pltpu.make_async_copy(info_v, info_all.at[tp], small_sem.at[0]).wait()
+                load = pltpu.make_async_copy(info_all, infos, small_sem.at[0])
+                load.start()
+                load.wait()
+                count = jnp.broadcast_to(token_count(), (1, 128))
+                for r in range(GROUPS):
+                    spread(info_v[1, r:r + 1, :].astype(f32) / count, slice(r * 128, (r + 1) * 128), scale_v)
 
         def step(t, c):
             @pl.when(t > 0)
@@ -331,18 +345,17 @@
                 stat_v[1, pl.ds(r, 1), :] = jnp.transpose(tgt)[0:1, :]
             return c
         lax.fori_loop(0, TOK // 512, finish, 0)
-        pltpu.make_async_copy(m_s, lse_b, wide_sem.at[0]).start()
-        pltpu.make_async_copy(info_v, info_all.at[tp], small_sem.at[0]).wait()
         for h in range(2):
             z_copy(last, h).wait()
+        z_load(zt, 0).start()
+        et_load(et, 0).start()
         half = e_all.at[pl.ds(0, ROWS // 2)]
         pltpu.make_async_copy(half, half, xs_send).wait()
         pltpu.make_async_copy(half, half, ys_send).wait()
         full = e_all.at[pl.ds(0, ROWS)]
         pltpu.make_async_copy(full, full, ds_send).wait()
         pltpu.make_async_copy(full, full, pe_send).wait()
-        own = pltpu.make_async_copy(stat_v, stat_all.at[tp], small_sem.at[1])
-        own.start()
+        pltpu.make_async_copy(stat_v, stat_all.at[tp], small_sem.at[1]).start()
         for p, dev in group:
             remote(stat_v, stat_all.at[tp], sm_send, stat_recv.at[p], dev).start()
 
@@ -351,14 +364,14 @@
             return c
         lax.fori_loop(1, XCHS, start_xt, 0)
         xp_copy.start()
-        own.wait()
-        for i, (src, dst) in enumerate(((m_s, lse_b), (mr_v.at[0], mean_b), (mr_v.at[1], rstd_b))):
-            pltpu.make_async_copy(src, dst, wide_sem.at[i]).wait()
-    bf16, f32 = jnp.bfloat16, jnp.float32
-    wide = pltpu.VMEM((TOK, 128), f32)
-    pl.run_scoped(forward, pltpu.VMEM((TOK, DIM), bf16), pltpu.VMEM((2, LN_ROWS, DIM), bf16), pltpu.VMEM((2, TILE, DIM), bf16),
-                  pltpu.VMEM((HB, TILE), f32), pltpu.VMEM((HB, TILE), f32), pltpu.VMEM((TOK, 128), jnp.int32), wide, wide, wide,
-                  pltpu.VMEM((2, TOK, 128), f32), pltpu.VMEM((2, 8, DIM), f32))
+
+    def z_load(zt, k):
+        slot = lax.rem(k, 2)
+        return pltpu.make_async_copy(z_out.at[:, pl.ds(pl.multiple_of(k * KT, KT), KT)], zt.at[slot], zt_sem.at[slot])
+
+    def et_load(et, k):
+        slot = lax.rem(k, 2)
+        return pltpu.make_async_copy(e_all.at[pl.ds(pl.multiple_of(k * KT, KT), KT)], et.at[slot], et_sem.at[slot])
 
     def dzt_copy(k):
         rows = pl.ds(pl.multiple_of(lax.rem(k, 4) * KT, KT), KT)
@@ -367,37 +380,12 @@
     def token_count():
         return jnp.sum(infos[:, 1].astype(f32))
 
-    def backward(acc):
-        def d_phase(zt, et, da, db, dzt, lse_v, scale_v, tcol_v):
-            lse_load = pltpu.make_async_copy(lse_b, lse_v, wide_sem.at[0])
-            lse_load.start()
-            for p, dev in group:
-                remote(info, info_all.at[tp], sm_send, info_recv.at[p], dev).wait_recv()
-            info_load = pltpu.make_async_copy(info_all, infos, small_sem.at[0])
-            info_load.start()
-
-            def z_load(k):
-                slot = lax.rem(k, 2)
-                return pltpu.make_async_copy(z_out.at[:, pl.ds(pl.multiple_of(k * KT, KT), KT)], zt.at[slot], z_sem.at[slot])
-
-            def e_load(k):
-                slot = lax.rem(k, 2)
-                return pltpu.make_async_copy(e_all.at[pl.ds(pl.multiple_of(k * KT, KT), KT)], et.at[slot], e_sem.at[slot])
-
+    def token_grads(lse_v, scale_v, tcol_v, mr, zt, et, acc):
+        def d_phase(da, db, dzt):
             def dzt_store(k, ref):
                 slot = lax.rem(k, 2)
                 return pltpu.make_async_copy(dzt.at[slot], ref.at[pl.ds(pl.multiple_of(lax.rem(k, 4) * KT, KT), KT)], eo_sem.at[slot])
-            z_load(0).start()
-            e_load(0).start()
-            acc[...] = jnp.zeros(acc.shape, jnp.float32)
-            info_load.wait()
-            lse_load.wait()
-            count = jnp.broadcast_to(token_count(), (1, 128))
-            for r in range(GROUPS):
-                rows = slice(r * 128, (r + 1) * 128)
-                spread(info_v[1, r:r + 1, :].astype(f32) / count, rows, scale_v)
-                spread(tcol[r:r + 1, :], rows, tcol_v)
-
+            acc[...] = jnp.zeros(acc.shape, f32)
             lane = lax.broadcasted_iota(jnp.int32, (PIECE, 128), 1)
 
             def piece(dst, rows, low, k, tie):
@@ -429,7 +417,7 @@
                         low = n * per
                         dzt[slot, :, base + low:base + low + 256] = jnp.transpose(src[low:low + 256, :])
 
-            z_load(0).wait()
+            z_load(zt, 0).wait()
 
             def first(i, c):
                 rows = pl.ds(pl.multiple_of(i * PIECE, PIECE), PIECE)
@@ -440,8 +428,8 @@
             def step(k, c):
                 @pl.when(k + 1 < VOCAB // KT)
                 def _():
-                    z_load(k + 1).start()
-                    e_load(k + 1).start()
+                    z_load(zt, k + 1).start()
+                    et_load(et, k + 1).start()
                 for at, j in WAIT_STEP.items():
                     @pl.when(k == at)
                     def _(j=j):
@@ -454,12 +442,12 @@
                 @pl.when((k >= 6) & (k < 10))
                 def _():
                     dzt_copy(k - 2).start()
-                e_load(k).wait()
+                et_load(et, k).wait()
                 half_step(k, da, db, 0, HB, k)
 
                 @pl.when(k + 1 < VOCAB // KT)
                 def _():
-                    z_load(k + 1).wait()
+                    z_load(zt, k + 1).wait()
                 half_step(k, db, da, HB, 0, k + 1)
 
                 @pl.when(k < 4)
@@ -472,30 +460,24 @@
                 return c
             lax.fori_loop(0, VOCAB // KT, step, 0)
         half = pltpu.VMEM((HB, KT), bf16)
-        pl.run_scoped(d_phase, pltpu.VMEM((2, TOK, KT), f32), pltpu.VMEM((2, KT, DIM), bf16), half, half, pltpu.VMEM((2, KT, TOK), bf16),
-                      pltpu.VMEM((TOK, 128), f32), pltpu.VMEM((TOK, 128), f32), pltpu.VMEM((TOK, 128), jnp.int32))
-
-        def n_phase(hb, ob, mr):
+        pl.run_scoped(d_phase, half, half, pltpu.VMEM((2, KT, TOK), bf16))
+
+        def n_phase(hb, ob):
             def h_load(i):
                 slot = lax.rem(i, 2)
-                return pltpu.make_async_copy(hid.at[pl.ds(pl.multiple_of(i * LN_ROWS, LN_ROWS), LN_ROWS)], hb.at[slot], z_sem.at[slot])
+                return pltpu.make_async_copy(hid.at[pl.ds(pl.multiple_of(i * NB_ROWS, NB_ROWS), NB_ROWS)], hb.at[slot], z_sem.at[slot])
 
             def o_store(i):
                 slot = lax.rem(i, 2)
-                return pltpu.make_async_copy(ob.at[slot], dhid.at[pl.ds(pl.multiple_of(i * LN_ROWS, LN_ROWS), LN_ROWS)], e_sem.at[slot])
-            mr_loads = [pltpu.make_async_copy(src, mr.at[i], wide_sem.at[i]) for i, src in enumerate((mean_b, rstd_b))]
-            for cp in mr_loads:
-                cp.start()
+                return pltpu.make_async_copy(ob.at[slot], dhid.at[pl.ds(pl.multiple_of(i * NB_ROWS, NB_ROWS), NB_ROWS)], e_sem.at[slot])
             h_load(0).start()
             gb_v[...] = jnp.zeros(gb_v.shape, jnp.float32)
             g8[...] = jnp.broadcast_to(gain[...], (8, DIM))
-            for cp in mr_loads:
-                cp.wait()
 
             def tile(i, c):
                 slot = lax.rem(i, 2)
 
-                @pl.when(i + 1 < TOK // LN_ROWS)
+                @pl.when(i + 1 < TOK // NB_ROWS)
                 def _():
                     h_load(i + 1).start()
 
@@ -508,7 +490,7 @@
                     units = range(NB_UNROLL)
                     base = r * 16 * NB_UNROLL
                     low = [pl.ds(pl.multiple_of(base + u * 16, 16), 16) for u in units]
-                    row = [pl.ds(pl.multiple_of(i * LN_ROWS + base + u * 16, 16), 16) for u in units]
+                    row = [pl.ds(pl.multiple_of(i * NB_ROWS + base + u * 16, 16), 16) for u in units]
                     zero = jnp.zeros((16, 128), jnp.float32)
                     sum1, sum3 = [zero] * NB_UNROLL, [zero] * NB_UNROLL
 
@@ -535,18 +517,18 @@
                             cols = slice(k * 128, (k + 1) * 128)
                             _, xhat, gx = load(u, cols)
                             ob[slot, low[u], cols] = (mr[1, row[u], :] * (gx - c1[u] - xhat * c3[u])).astype(jnp.bfloat16)
-                            acc[row[u], cols] = zero
                     return c2
-                lax.fori_loop(0, LN_ROWS // (16 * NB_UNROLL), rows_body, 0)
+                lax.fori_loop(0, NB_ROWS // (16 * NB_UNROLL), rows_body, 0)
                 o_store(i).start()
                 return c
-            lax.fori_loop(0, TOK // LN_ROWS, tile, 0)
+            lax.fori_loop(0, TOK // NB_ROWS, tile, 0)
             for i in range(2):
-                o_store(TOK // LN_ROWS - 2 + i).wait()
+                o_store(TOK // NB_ROWS - 2 + i).wait()
             gs_v[0:1, :] = jnp.sum(gb_v[0], axis=0, keepdims=True)
             gs_v[1:2, :] = jnp.sum(gb_v[1], axis=0, keepdims=True)
-        pl.run_scoped(n_phase, pltpu.VMEM((2, LN_ROWS, DIM), jnp.bfloat16), pltpu.VMEM((2, LN_ROWS, DIM), jnp.bfloat16),
-                      pltpu.VMEM((2, TOK, 128), jnp.float32))
+        pl.run_scoped(n_phase, pltpu.VMEM((2, NB_ROWS, DIM), bf16), pltpu.VMEM((2, NB_ROWS, DIM), bf16))
+
+    def weight_grads(acc):
         own = pltpu.make_async_copy(gs_v, gsum_all.at[tp], g_sem)
         xt_event(3)
 
@@ -581,6 +563,7 @@
                 lax.fori_loop(0, HBS, mul, 0)
 
             start_local(0)
+            acc[...] = jnp.zeros(acc.shape, f32)
 
             def rem_load(r):
                 slot = lax.rem(r, 2)
@@ -609,7 +592,7 @@
                     for p, dev in group:
                         remote(gs_v, gsum_all.at[tp], g_send, g_recv.at[p], dev).start()
 
-                @pl.when(i == 4)
+                @pl.when(i == 5)
                 def _():
                     xt_event(4)
 
@@ -630,6 +613,7 @@
             eo_load.wait()
             for p, dev in group:
                 remote(stat_v, stat_all.at[tp], sm_send, stat_recv.at[p], dev).wait_recv()
+            pltpu.make_async_copy(stat_v, stat_all.at[tp], small_sem.at[1]).wait()
             stat_load = pltpu.make_async_copy(stat_all, stats, small_sem.at[1])
             stat_load.start()
             stat_load.wait()
@@ -642,19 +626,15 @@
                 def _():
                     xt_event(5)
 
-                @pl.when(r == 3)
+                @pl.when(r == 4)
                 def _():
                     xt_event(6)
 
-                @pl.when(r == 6)
-                def _():
-                    xt_event(7)
-
-                @pl.when(r + 1 < XCHS)
-                def _():
+                def fetch():
                     xd_copy(r + 1).wait_recv()
                     for cp in rem_load(r + 1):
                         cp.start()
+                pl.when(r < XCHS - 2)(fetch)
                 x_load(x_out, 0, slot).wait()
 
                 @pl.when(r == XCHS - DEFER)
@@ -687,6 +667,11 @@
                     return c2
                 lax.fori_loop(0, ROWS // ZB, logits, 0)
 
+                @pl.when(r == XCHS - 2)
+                def _():
+                    xt_event(XCHS - 1)
+                    fetch()
+
                 @pl.when(r < XCHS - DEFER)
                 def _():
                     def mul(h, c2):
@@ -714,7 +699,19 @@
                       pltpu.VMEM((2, ROWS, KT), jnp.bfloat16), pltpu.VMEM((ZB, KT), jnp.float32))
 
         own.wait()
-    pl.run_scoped(backward, pltpu.VMEM((TOK, DIM), f32))
+
+    wide = pltpu.VMEM((TOK, 128), f32)
+    big = pltpu.VMEM((TOK, DIM), f32)
+
+    def tokens(m_s, scale_v, tc_v, mr_v, zt, et):
+        kept = (m_s, scale_v, tc_v, mr_v, zt, et)
+        pl.run_scoped(functools.partial(forward, *kept), pltpu.VMEM((TOK, DIM), bf16), pltpu.VMEM((2, LN_ROWS, DIM), bf16),
+                      pltpu.VMEM((2, TILE, DIM), bf16), pltpu.VMEM((HB, TILE), f32), pltpu.VMEM((HB, TILE), f32), wide, wide,
+                      pltpu.VMEM((2, 8, DIM), f32))
+        pl.run_scoped(functools.partial(token_grads, *kept), big)
+    pl.run_scoped(tokens, wide, wide, pltpu.VMEM((TOK, 128), jnp.int32), pltpu.VMEM((2, TOK, 128), f32),
+                  pltpu.VMEM((2, TOK, KT), f32), pltpu.VMEM((2, KT, DIM), bf16))
+    pl.run_scoped(weight_grads, big)
 
     pltpu.make_async_copy(x_out, x_out, xt_send).wait()
     pltpu.make_async_copy(x_out, x_out, xd_send).wait()
@@ -726,45 +723,47 @@
         remote(gs_v, gsum_all.at[tp], g_send, g_recv.at[p], dev).wait()
 
 
-def run_step(hidden, gain, bias, embed, tcol, info):
+def run_step(hidden, gain, bias, embed, info):
     any_spec = pl.BlockSpec(memory_space=pl.ANY)
     vmem_spec = pl.BlockSpec(memory_space=pltpu.VMEM)
     f32, bf16, i32 = jnp.float32, jnp.bfloat16, jnp.int32
     dma = pltpu.SemaphoreType.DMA
-    small = (4, 2, GROUPS, 128)
-    wide = ((TOK, 128), f32)
+    small, ints = (4, 2, GROUPS, 128), (4, 3, GROUPS, 128)
     mat, square = ((TOK, DIM), bf16), ((ROWS, TOK), bf16)
-    shapes = [((VOCAB, DIM), bf16), mat, ((TOK, VOCAB), f32), (small, f32), (small, i32), wide, wide, wide,
+    shapes = [((VOCAB, DIM), bf16), mat, ((TOK, VOCAB), f32), (small, f32), (ints, i32),
               mat, mat, mat, mat, square, square, square, ((2, ROWS, DEFER * XCH), bf16), ((ROWS, DIM), f32), ((4, 2, DIM), f32)]
     return pl.pallas_call(
         step_kernel,
         name="step",
         out_shape=[jax.ShapeDtypeStruct(s, d) for s, d in shapes],
-        in_specs=[any_spec, vmem_spec, vmem_spec, any_spec, vmem_spec, any_spec],
+        in_specs=[any_spec, vmem_spec, vmem_spec, any_spec, any_spec],
         out_specs=[any_spec] * len(shapes),
         scratch_shapes=[
-            pltpu.VMEM((2, GROUPS, 128), i32), pltpu.VMEM((2, GROUPS, 128), f32), pltpu.VMEM(small, f32), pltpu.VMEM(small, i32),
+            pltpu.VMEM((3, GROUPS, 128), i32), pltpu.VMEM((2, GROUPS, 128), f32), pltpu.VMEM(small, f32), pltpu.VMEM(ints, i32),
             pltpu.VMEM((2, 8, DIM), f32), pltpu.VMEM((2, DIM), f32), pltpu.VMEM((8, DIM), f32),
-            dma((2,)), dma, dma((2,)), dma((2,)), dma((2,)), dma((2,)), dma((3,)), dma((2,)), dma, dma,
+            dma((2,)), dma, dma((2,)), dma((2,)), dma((2,)), dma((2,)), dma((2,)), dma((2,)), dma((2,)), dma, dma,
             dma, dma, dma, dma, dma, dma, dma, dma, dma, dma,
-            dma((CHUNKS,)), dma((CHUNKS,)), dma((TILES // 2,)), dma((4,)), dma((4,)), dma((4,)),
+            dma((CHUNKS,)), dma((CHUNKS,)), dma((TILES - NEAR,)), dma((ROWS // PE_ROWS,)), dma((4,)), dma((4,)),
             dma((XCHS,)), dma((XCHS,)), dma, dma((4,)), dma((4,)),
         ],
         compiler_params=pltpu.CompilerParams(collective_id=0, has_side_effects=True, vmem_limit_bytes=67043328),
         cost_estimate=pl.CostEstimate(flops=12 * TOK * VOCAB * DIM, bytes_accessed=700 * 2 ** 20, transcendentals=3 * TOK * VOCAB),
-    )(hidden, gain, bias, embed, tcol, info)
+    )(hidden, gain, bias, embed, info)
 
 
 def finish_kernel(*refs):
     nb = DEFER * XCH // KT
     de_in, dz0, dz1 = refs[:3]
     xs = refs[3:3 + 2 * nb]
-    dh_in, stat_all, info_all, gsum_all, de_out, dh_out, loss, mean, sums = refs[3 + 2 * nb:]
-    prod = de_in[...]
-    for b in range(nb):
-        prod = prod + jnp.dot(dz0[0, :, b * KT:(b + 1) * KT], xs[b][...], preferred_element_type=jnp.float32)
-        prod = prod + jnp.dot(dz1[0, :, b * KT:(b + 1) * KT], xs[nb + b][...], preferred_element_type=jnp.float32)
-    de_out[...] = prod
+    dh_in, stat_all, info_all, gsum_all, de_out, dh_out, loss, mean, d_gain, d_bias = refs[3 + 2 * nb:]
+    for h in range(HBS):
+        rows = slice(h * HB, (h + 1) * HB)
+        prod = None
+        for b in range(nb):
+            for dz, x in ((dz0, xs[b]), (dz1, xs[nb + b])):
+                part = jnp.dot(dz[0, rows, b * KT:(b + 1) * KT], x[...], preferred_element_type=jnp.float32)
+                prod = part if prod is None else prod + part
+        de_out[rows, :] = de_in[rows, :] + prod
     dh_out[...] = dh_in[...]
 
     @pl.when(pl.program_id(0) == 0)
@@ -773,8 +772,10 @@
         all_loss = (stat_all[:, 0] - stat_all[:, 1]) * weights
         tp = lax.axis_index('tp')
         loss[...] = (stat_all[tp, 0] - stat_all[tp, 1]) * info_all[tp, 1].astype(jnp.float32)
-        mean[...] = jnp.broadcast_to(jnp.sum(all_loss), (1, 128)) / jnp.broadcast_to(jnp.sum(weights), (1, 128))
-        sums[...] = ((gsum_all[0] + gsum_all[1]) + gsum_all[2]) + gsum_all[3]
+        mean[...] = jnp.broadcast_to(jnp.sum(all_loss), (1, 1)) / jnp.broadcast_to(jnp.sum(weights), (1, 1))
+        sums = ((gsum_all[0] + gsum_all[1]) + gsum_all[2]) + gsum_all[3]
+        d_gain[...] = sums[0:1]
+        d_bias[...] = sums[1:2]
 
 
 def finish(de_part, dzt_last, x_xp, x_xq, dhid, stat_all, info_all, gsum_all):
@@ -789,7 +790,7 @@
     def whole(shape):
         return pl.BlockSpec(shape, lambda i: (0,) * len(shape))
     nb = len(x_specs)
-    outs = [((ROWS, DIM), jnp.float32), ((TOK, DIM), jnp.bfloat16), ((GROUPS, 128), jnp.float32), ((1, 128), jnp.float32), ((2, DIM), jnp.float32)]
+    outs = [((ROWS, DIM), jnp.float32), ((TOK, DIM), jnp.bfloat16), ((GROUPS, 128), jnp.float32), ((1, 1), jnp.float32), ((1, DIM), jnp.float32), ((1, DIM), jnp.float32)]
     return pl.pallas_call(
         finish_kernel,
         name="finish",
@@ -804,7 +805,7 @@
             whole(stat_all.shape), whole(info_all.shape), whole(gsum_all.shape),
         ],
         out_specs=[pl.BlockSpec((ROWS, cols), lambda i: (0, i)), pl.BlockSpec((rows, DIM), lambda i: (i, 0)),
-                   whole((GROUPS, 128)), whole((1, 128)), whole((2, DIM))],
+                   whole((GROUPS, 128)), whole((1, 1)), whole((1, DIM)), whole((1, DIM))],
         compiler_params=pltpu.CompilerParams(vmem_limit_bytes=60 * 1024 * 1024),
         cost_estimate=pl.CostEstimate(flops=4 * ROWS * DIM * depth, bytes_accessed=120 * 2 ** 20, transcendentals=0),
     )(de_part, dzt_last, dzt_last, *[x_xp] * nb, *[x_xq] * nb, dhid, stat_all, info_all, gsum_all)
@@ -813,19 +814,19 @@
 def solution(mesh):
     def body(hidden, ln_gain, ln_bias, embed, targets, loss_mask):
         dp, rank = lax.axis_index('dp'), lax.axis_index('tp')
-        info = jnp.stack([targets, loss_mask]).reshape(2, GROUPS, 128)
         shard = targets // ROWS
         block = jnp.bitwise_xor(shard, rank)
         row = targets % ROWS
         half = row // (ROWS // 2)
         sub = row % (ROWS // 2)
         piece = (block - 2) * 2 + jnp.bitwise_xor(half, dp)
-        far = 2 * ROWS + (sub // 128) * TILE + piece * 128 + sub % 128
-        tcol = jnp.where(block < 2, block * ROWS + row, far).reshape(GROUPS, 128)
-        outs = run_step(hidden, ln_gain.reshape(1, DIM), ln_bias.reshape(1, DIM), embed, tcol, info)
-        stat_all, info_all, dhid, x_xp, x_xq, dzt_last, de_part, gsum_all = (outs[i] for i in (3, 4, 8, 10, 11, 15, 16, 17))
-        d_embed, d_hidden, loss, mean, sums = finish(de_part, dzt_last, x_xp, x_xq, dhid, stat_all, info_all, gsum_all)
-        return loss.reshape(TOK), mean[0, :1], d_hidden, d_embed, sums[0], sums[1]
+        far = 2 * ROWS + (sub // PIECE_ROWS) * TILE + piece * PIECE_ROWS + sub % PIECE_ROWS
+        tcol = jnp.where(block < 2, block * ROWS + row, far)
+        info = jnp.stack([targets, loss_mask, tcol]).reshape(3, GROUPS, 128)
+        outs = run_step(hidden, ln_gain.reshape(1, DIM), ln_bias.reshape(1, DIM), embed, info)
+        stat_all, info_all, dhid, x_xp, x_xq, dzt_last, de_part, gsum_all = (outs[i] for i in (3, 4, 5, 7, 8, 12, 13, 14))
+        d_embed, d_hidden, loss, mean, d_gain, d_bias = finish(de_part, dzt_last, x_xp, x_xq, dhid, stat_all, info_all, gsum_all)
+        return loss.reshape(TOK), mean.reshape(1), d_hidden, d_embed, d_gain.reshape(DIM), d_bias.reshape(DIM)
 
     token_rows = P(('dp', 'tp'))
     token_mat = P(('dp', 'tp'), None)

time: 662 us -> 649 us (0.980)
  Pallas kernels: 657 us -> 645 us
    pallas_call x1, Pallas kernels: 607 us -> 595 us  [run_step(): pl.pallas_call(step_kernel, name='step', out_shape=[jax.ShapeDtypeStruct(...]
where the time goes in v3:
time: 649 us; the launch traced here: 648 us
  Pallas kernels  645 us (99%)
    pallas_call x1, Pallas kernels, run_step(): pl.pallas_call(step_kernel, name='step', out_shape=[jax.ShapeDtypeStruct(...  595 us
    pallas_call x1, Pallas kernels, finish(): pl.pallas_call(finish_kernel, name='finish', grid=(steps,), out_shape=[ja...  49.8 us

profile of v3, /device:TPU:0, one launch (start us, length us, event | category | flops | bytes accessed | tf_op | source)
XLA Modules:
  0.0 647.6 jit_solution(8147513513123137280)
XLA Ops:
  0.6 0.7 fusion.6
  1.4 1.3 pad_add_fusion.info
  2.7 594.9 %step.1 = (bf16[8192,4096]{1,0:T(8,128)(2,1)}, bf16[2048,4096]{1,0:T(8,128)(2,1)}, f32[2048,8192]{1,0:T(8,128)}, f32[4,2,16,128]{3,2,1,0:T(8,128)}, s32[4,3,16,1...) custom-call(bf16[2048,4096]{1,0:T(8,128)(2,1)} %hid.1, ...), custom_call_target="tpu_custom_call" | custom-call | flops 824633720832 | bytes 734003200 | tf_op jit(solution)/shard_map/step/pallas_call | solution.py:735
  597.6 49.8 %finish.1 = (f32[2048,4096]{1,0:T(8,128)}, bf16[2048,4096]{1,0:T(8,128)(2,1)}, f32[16,128]{1,0:T(8,128)}, f32[1,1]{1,0:T(1,128)}, f32[1,4096]{1,0:T(1,128)}, /*index=5*/f32[1,4096]{1,0:T(1,128)}) custom-call(f32[2048,4096]{1,0:T(8,128)} %get-tuple-element.20.refs_0_, bf16[2,2048,1024]{2,1,0:T(8,128)(2,1)} %get-tuple-element.21.refs_1_.refs_2_, ...), custom_call_target="tpu_custom_call" | custom-call | flops 34359738368 | bytes 125829120 | tf_op jit(solution)/shard_map/finish/pallas_call | solution.py:794

commit v4 on v3

--- a/solution.py
+++ b/solution.py
@@ -30,7 +30,7 @@
 XCH = 256
 XCHS = TOK // XCH
 KT = 512
-DEFER = 4
+DEFER = 6
 WAIT_STEP = {4: 0, 9: 1, 14: 2}
 ZB = 512
 NCOL = 512
@@ -626,7 +626,7 @@
                 def _():
                     xt_event(5)
 
-                @pl.when(r == 4)
+                @pl.when(r == 5)
                 def _():
                     xt_event(6)
 

time: 649 us -> 651 us (level)
    pallas_call x1, Pallas kernels: 49.8 us -> 65.6 us  [finish(): pl.pallas_call(finish_kernel, name='finish', grid=(steps,), out_shape=[ja...]
    pallas_call x1, Pallas kernels: 595 us -> 582 us  [run_step(): pl.pallas_call(step_kernel, name='step', out_shape=[jax.ShapeDtypeStruct(...]
where the time goes in v4:
time: 651 us; the launch traced here: 650 us
  Pallas kernels  647 us (99%)
    pallas_call x1, Pallas kernels, run_step(): pl.pallas_call(step_kernel, name='step', out_shape=[jax.ShapeDtypeStruct(...  582 us
    pallas_call x1, Pallas kernels, finish(): pl.pallas_call(finish_kernel, name='finish', grid=(steps,), out_shape=[ja...  65.6 us

profile of v4, /device:TPU:0, one launch (start us, length us, event | category | flops | bytes accessed | tf_op | source)
XLA Modules:
  0.0 650.2 jit_solution(5772995414647237376)
XLA Ops:
  0.6 0.7 fusion.6
  1.4 1.3 pad_add_fusion.info
  2.7 581.7 %step.1 = (bf16[8192,4096]{1,0:T(8,128)(2,1)}, bf16[2048,4096]{1,0:T(8,128)(2,1)}, f32[2048,8192]{1,0:T(8,128)}, f32[4,2,16,128]{3,2,1,0:T(8,128)}, s32[4,3,16,1...) custom-call(bf16[2048,4096]{1,0:T(8,128)(2,1)} %hid.1, ...), custom_call_target="tpu_custom_call" | custom-call | flops 824633720832 | bytes 734003200 | tf_op jit(solution)/shard_map/step/pallas_call | solution.py:735
  584.4 65.6 %finish.1 = (f32[2048,4096]{1,0:T(8,128)}, bf16[2048,4096]{1,0:T(8,128)(2,1)}, f32[16,128]{1,0:T(8,128)}, f32[1,1]{1,0:T(1,128)}, f32[1,4096]{1,0:T(1,128)}, /*index=5*/f32[1,4096]{1,0:T(1,128)}) custom-call(f32[2048,4096]{1,0:T(8,128)} %get-tuple-element.20.refs_0_, bf16[2,2048,1536]{2,1,0:T(8,128)(2,1)} %get-tuple-element.21.refs_1_.refs_2_, ...), custom_call_target="tpu_custom_call" | custom-call | flops 51539607552 | bytes 125829120 | tf_op jit(solution)/shard_map/finish/pallas_call | solution.py:794

commit v5 on v3

--- a/solution.py
+++ b/solution.py
@@ -30,12 +30,12 @@
 XCH = 256
 XCHS = TOK // XCH
 KT = 512
-DEFER = 4
+DEFER = 2
 WAIT_STEP = {4: 0, 9: 1, 14: 2}
 ZB = 512
 NCOL = 512
 KCOL = 1024
-NB_UNROLL = 8
+NB_UNROLL = 4
 NB_ROWS = 128
 GROUPS = TOK // 128
 NT = (((1,), (1,)), ((), ()))
@@ -347,7 +347,8 @@
         lax.fori_loop(0, TOK // 512, finish, 0)
         for h in range(2):
             z_copy(last, h).wait()
-        z_load(zt, 0).start()
+        for k, h in ((0, 0), (1, 0), (0, 1)):
+            z_load(zt, k, h).start()
         et_load(et, 0).start()
         half = e_all.at[pl.ds(0, ROWS // 2)]
         pltpu.make_async_copy(half, half, xs_send).wait()
@@ -365,9 +366,11 @@
         lax.fori_loop(1, XCHS, start_xt, 0)
         xp_copy.start()
 
-    def z_load(zt, k):
+    def z_load(zt, k, h):
         slot = lax.rem(k, 2)
-        return pltpu.make_async_copy(z_out.at[:, pl.ds(pl.multiple_of(k * KT, KT), KT)], zt.at[slot], zt_sem.at[slot])
+        rows = slice(h * HB, (h + 1) * HB)
+        return pltpu.make_async_copy(
+            z_out.at[rows, pl.ds(pl.multiple_of(k * KT, KT), KT)], zt.at[slot, rows], zt_sem.at[2 * h + slot])
 
     def et_load(et, k):
         slot = lax.rem(k, 2)
@@ -385,7 +388,6 @@
             def dzt_store(k, ref):
                 slot = lax.rem(k, 2)
                 return pltpu.make_async_copy(dzt.at[slot], ref.at[pl.ds(pl.multiple_of(lax.rem(k, 4) * KT, KT), KT)], eo_sem.at[slot])
-            acc[...] = jnp.zeros(acc.shape, f32)
             lane = lax.broadcasted_iota(jnp.int32, (PIECE, 128), 1)
 
             def piece(dst, rows, low, k, tie):
@@ -408,7 +410,7 @@
                 for n in range(DIM // NCOL):
                     cols = slice(n * NCOL, (n + 1) * NCOL)
                     prod = jnp.dot(src[...], et[slot, :, cols], preferred_element_type=f32)
-                    acc[base:base + HB, cols] += prod
+                    acc[base:base + HB, cols] = jnp.where(k == 0, 0.0, acc[base:base + HB, cols]) + prod
                     for q in range(0, per, PIECE):
                         at = q * HB // per
                         low = n * per + q
@@ -417,7 +419,7 @@
                         low = n * per
                         dzt[slot, :, base + low:base + low + 256] = jnp.transpose(src[low:low + 256, :])
 
-            z_load(zt, 0).wait()
+            z_load(zt, 0, 0).wait()
 
             def first(i, c):
                 rows = pl.ds(pl.multiple_of(i * PIECE, PIECE), PIECE)
@@ -426,10 +428,15 @@
             lax.fori_loop(0, HB // PIECE, first, 0)
 
             def step(k, c):
+                @pl.when(k + 2 < VOCAB // KT)
+                def _():
+                    z_load(zt, k + 2, 0).start()
+
                 @pl.when(k + 1 < VOCAB // KT)
                 def _():
-                    z_load(zt, k + 1).start()
+                    z_load(zt, k + 1, 1).start()
                     et_load(et, k + 1).start()
+                    z_load(zt, k + 1, 0).wait()
                 for at, j in WAIT_STEP.items():
                     @pl.when(k == at)
                     def _(j=j):
@@ -443,11 +450,8 @@
                 def _():
                     dzt_copy(k - 2).start()
                 et_load(et, k).wait()
+                z_load(zt, k, 1).wait()
                 half_step(k, da, db, 0, HB, k)
-
-                @pl.when(k + 1 < VOCAB // KT)
-                def _():
-                    z_load(zt, k + 1).wait()
                 half_step(k, db, da, HB, 0, k + 1)
 
                 @pl.when(k < 4)
@@ -510,13 +514,19 @@
                             d_bias = d_bias + (dx[0:8] + dx[8:16])
                         gb_v[0, :, cols] = d_gain
                         gb_v[1, :, cols] = d_bias
-                    c1 = [jnp.broadcast_to(jnp.sum(v, axis=-1, keepdims=True) * (1.0 / DIM), (16, 128)) for v in sum1]
-                    c3 = [jnp.broadcast_to(jnp.sum(v, axis=-1, keepdims=True) * (1.0 / DIM), (16, 128)) for v in sum3]
+                    slope, shift = [], []
                     for u in units:
+                        mean, rstd = mr[0, row[u], :], mr[1, row[u], :]
+                        c1 = jnp.broadcast_to(jnp.sum(sum1[u], axis=-1, keepdims=True) * (1.0 / DIM), (16, 128))
+                        c3 = jnp.broadcast_to(jnp.sum(sum3[u], axis=-1, keepdims=True) * (1.0 / DIM), (16, 128))
+                        slope.append(c3 * rstd * rstd)
+                        shift.append(slope[u] * mean - c1 * rstd)
+                    for u in units:
+                        rstd = mr[1, row[u], :]
                         for k in range(DIM // 128):
                             cols = slice(k * 128, (k + 1) * 128)
-                            _, xhat, gx = load(u, cols)
-                            ob[slot, low[u], cols] = (mr[1, row[u], :] * (gx - c1[u] - xhat * c3[u])).astype(jnp.bfloat16)
+                            gx = acc[row[u], cols] * jnp.concatenate([g8[:, cols]] * 2, axis=0)
+                            ob[slot, low[u], cols] = (gx * rstd - hb[slot, low[u], cols].astype(f32) * slope[u] + shift[u]).astype(bf16)
                     return c2
                 lax.fori_loop(0, NB_ROWS // (16 * NB_UNROLL), rows_body, 0)
                 o_store(i).start()
@@ -530,9 +540,8 @@
 
     def weight_grads(acc):
         own = pltpu.make_async_copy(gs_v, gsum_all.at[tp], g_sem)
-        xt_event(3)
-
-        def e_phase(eo, xt, dzb, zs):
+
+        def e_phase(eo, xt, dzb, zs, z1):
             eo_load = pltpu.make_async_copy(emb, eo, big_sem)
 
             def x_load(ref, row, slot):
@@ -554,16 +563,13 @@
                     x_load(x_part, (i - 4) * KT, slot).start()
                     dz_load(dzt_part, (i - 4) * KT, slot).start()
 
-            def add(slot):
-                def mul(h, c2):
-                    rows = pl.ds(pl.multiple_of(h * HB, HB), HB)
+            def add(slot, first):
+                for rows in (slice(0, HB), slice(HB, TOK)):
                     for n in range(0, DIM, NCOL):
-                        acc[rows, n:n + NCOL] += jnp.dot(dzb[slot, rows, :], xt[slot, :, n:n + NCOL], preferred_element_type=jnp.float32)
-                    return c2
-                lax.fori_loop(0, HBS, mul, 0)
+                        prod = jnp.dot(dzb[slot, rows, :], xt[slot, :, n:n + NCOL], preferred_element_type=f32)
+                        acc[rows, n:n + NCOL] = jnp.where(first, 0.0, acc[rows, n:n + NCOL]) + prod
 
             start_local(0)
-            acc[...] = jnp.zeros(acc.shape, f32)
 
             def rem_load(r):
                 slot = lax.rem(r, 2)
@@ -592,7 +598,11 @@
                     for p, dev in group:
                         remote(gs_v, gsum_all.at[tp], g_send, g_recv.at[p], dev).start()
 
-                @pl.when(i == 5)
+                @pl.when(i == 1)
+                def _():
+                    xt_event(3)
+
+                @pl.when(i == 6)
                 def _():
                     xt_event(4)
 
@@ -607,7 +617,7 @@
                         cp.start()
                 x_load(x_out, 0, slot).wait()
                 dz_load(dzt_own, 0, slot).wait()
-                add(slot)
+                add(slot, i == 0)
                 return c
             lax.fori_loop(0, 8, local, 0)
             eo_load.wait()
@@ -622,7 +632,7 @@
             def far(r, c):
                 slot = lax.rem(r, 2)
 
-                @pl.when(r == 1)
+                @pl.when(r == 2)
                 def _():
                     xt_event(5)
 
@@ -652,20 +662,28 @@
                     at = pl.ds(2 * r + g % 2, 1)
                     far_rows.append((stats[who, 0, at, :], infos[who, 1, at, :].astype(f32) / count, infos[who, 0, at, :] - tp * ROWS))
 
-                def logits(h, c2):
-                    for k in range(0, DIM, KCOL):
-                        prod = lax.dot_general(eo[pl.ds(pl.multiple_of(h * ZB, ZB), ZB), k:k + KCOL], xt[slot, :, k:k + KCOL], NT, preferred_element_type=jnp.float32)
-                        zs[...] = prod if k == 0 else zs[...] + prod
-                    for q in range(ZB // 32):
-                        row = h * ZB + q * 32
-                        line = lax.broadcasted_iota(jnp.int32, (32, 128), 0)
-                        for g, (lse, scale, trel) in enumerate(far_rows):
-                            cols = slice(g * 128, (g + 1) * 128)
-                            hot = ((trel - row) == line).astype(f32)
-                            val = (jnp.exp(zs[q * 32:(q + 1) * 32, cols] - lse) - hot) * scale
-                            dzb[slot, pl.ds(pl.multiple_of(row, 32), 32), cols] = val.astype(bf16)
+                def logits(h2, c2):
+                    def multiply(h, z):
+                        for k in range(0, DIM, KCOL):
+                            prod = lax.dot_general(eo[pl.ds(pl.multiple_of(h * ZB, ZB), ZB), k:k + KCOL], xt[slot, :, k:k + KCOL], NT, preferred_element_type=jnp.float32)
+                            z[...] = prod if k == 0 else z[...] + prod
+
+                    def convert(h, z):
+                        for q in range(ZB // 32):
+                            row = h * ZB + q * 32
+                            line = lax.broadcasted_iota(jnp.int32, (32, 128), 0)
+                            for g, (lse, scale, trel) in enumerate(far_rows):
+                                cols = slice(g * 128, (g + 1) * 128)
+                                hot = ((trel - row) == line).astype(f32)
+                                val = (jnp.exp(z[q * 32:(q + 1) * 32, cols] - lse) - hot) * scale
+                                dzb[slot, pl.ds(pl.multiple_of(row, 32), 32), cols] = val.astype(bf16)
+                    lo, hi = 2 * h2, 2 * h2 + 1
+                    multiply(lo, zs)
+                    multiply(hi, z1)
+                    convert(lo, zs)
+                    convert(hi, z1)
                     return c2
-                lax.fori_loop(0, ROWS // ZB, logits, 0)
+                lax.fori_loop(0, ROWS // (2 * ZB), logits, 0)
 
                 @pl.when(r == XCHS - 2)
                 def _():
@@ -696,7 +714,7 @@
                 dz_out(0, 1, slot).wait()
             pltpu.make_async_copy(acc, de_part, big_sem).wait()
         pl.run_scoped(e_phase, pltpu.VMEM((ROWS, DIM), jnp.bfloat16), pltpu.VMEM((2, KT, DIM), jnp.bfloat16),
-                      pltpu.VMEM((2, ROWS, KT), jnp.bfloat16), pltpu.VMEM((ZB, KT), jnp.float32))
+                      pltpu.VMEM((2, ROWS, KT), jnp.bfloat16), pltpu.VMEM((ZB, KT), jnp.float32), pltpu.VMEM((ZB, KT), jnp.float32))
 
         own.wait()
 
@@ -741,7 +759,7 @@
         scratch_shapes=[
             pltpu.VMEM((3, GROUPS, 128), i32), pltpu.VMEM((2, GROUPS, 128), f32), pltpu.VMEM(small, f32), pltpu.VMEM(ints, i32),
             pltpu.VMEM((2, 8, DIM), f32), pltpu.VMEM((2, DIM), f32), pltpu.VMEM((8, DIM), f32),
-            dma((2,)), dma, dma((2,)), dma((2,)), dma((2,)), dma((2,)), dma((2,)), dma((2,)), dma((2,)), dma, dma,
+            dma((2,)), dma, dma((2,)), dma((2,)), dma((2,)), dma((4,)), dma((2,)), dma((2,)), dma((2,)), dma, dma,
             dma, dma, dma, dma, dma, dma, dma, dma, dma, dma,
             dma((CHUNKS,)), dma((CHUNKS,)), dma((TILES - NEAR,)), dma((ROWS // PE_ROWS,)), dma((4,)), dma((4,)),
             dma((XCHS,)), dma((XCHS,)), dma, dma((4,)), dma((4,)),

time: 649 us -> 654 us (level)
    pallas_call x1, Pallas kernels: 595 us -> 608 us  [run_step(): pl.pallas_call(step_kernel, name='step', out_shape=[jax.ShapeDtypeStruct(...]
    pallas_call x1, Pallas kernels: 49.8 us -> 42.3 us  [finish(): pl.pallas_call(finish_kernel, name='finish', grid=(steps,), out_shape=[ja...]
where the time goes in v5:
time: 654 us; the launch traced here: 653 us
  Pallas kernels  650 us (99%)
    pallas_call x1, Pallas kernels, run_step(): pl.pallas_call(step_kernel, name='step', out_shape=[jax.ShapeDtypeStruct(...  608 us
    pallas_call x1, Pallas kernels, finish(): pl.pallas_call(finish_kernel, name='finish', grid=(steps,), out_shape=[ja...  42.3 us

profile of v5, /device:TPU:0, one launch (start us, length us, event | category | flops | bytes accessed | tf_op | source)
XLA Modules:
  0.0 652.8 jit_solution(10386491401583033453)
XLA Ops:
  0.6 0.7 fusion.6
  1.4 1.3 pad_add_fusion.info
  2.7 607.6 %step.1 = (bf16[8192,4096]{1,0:T(8,128)(2,1)}, bf16[2048,4096]{1,0:T(8,128)(2,1)}, f32[2048,8192]{1,0:T(8,128)}, f32[4,2,16,128]{3,2,1,0:T(8,128)}, s32[4,3,16,1...) custom-call(bf16[2048,4096]{1,0:T(8,128)(2,1)} %hid.1, ...), custom_call_target="tpu_custom_call" | custom-call | flops 824633720832 | bytes 734003200 | tf_op jit(solution)/shard_map/step/pallas_call | solution.py:753
  610.3 42.3 %finish.1 = (f32[2048,4096]{1,0:T(8,128)}, bf16[2048,4096]{1,0:T(8,128)(2,1)}, f32[16,128]{1,0:T(8,128)}, f32[1,1]{1,0:T(1,128)}, f32[1,4096]{1,0:T(1,128)}, /*index=5*/f32[1,4096]{1,0:T(1,128)}) custom-call(f32[2048,4096]{1,0:T(8,128)} %get-tuple-element.20.refs_0_, bf16[2,2048,512]{2,1,0:T(8,128)(2,1)} %get-tuple-element.21.refs_1_.refs_2_, ...), custom_call_target="tpu_custom_call" | custom-call | flops 17179869184 | bytes 125829120 | tf_op jit(solution)/shard_map/finish/pallas_call | solution.py:812

commit v6 on v3

--- a/solution.py
+++ b/solution.py
@@ -35,8 +35,8 @@
 ZB = 512
 NCOL = 512
 KCOL = 1024
-NB_UNROLL = 8
-NB_ROWS = 128
+NB_UNROLL = 4
+NB_ROWS = 256
 GROUPS = TOK // 128
 NT = (((1,), (1,)), ((), ()))
 
@@ -294,6 +294,12 @@
             def _():
                 p_event(t - (NEAR - 1))
 
+            @pl.when(t == TILES - 2)
+            def _():
+                for k, h in ((0, 0), (1, 0), (0, 1)):
+                    z_load(zt, k, h).start()
+                et_load(et, 0).start()
+
             @pl.when(t == NEAR + 1)
             def _():
                 for p, dev in group:
@@ -347,8 +353,6 @@
         lax.fori_loop(0, TOK // 512, finish, 0)
         for h in range(2):
             z_copy(last, h).wait()
-        z_load(zt, 0).start()
-        et_load(et, 0).start()
         half = e_all.at[pl.ds(0, ROWS // 2)]
         pltpu.make_async_copy(half, half, xs_send).wait()
         pltpu.make_async_copy(half, half, ys_send).wait()
@@ -365,9 +369,11 @@
         lax.fori_loop(1, XCHS, start_xt, 0)
         xp_copy.start()
 
-    def z_load(zt, k):
+    def z_load(zt, k, h):
         slot = lax.rem(k, 2)
-        return pltpu.make_async_copy(z_out.at[:, pl.ds(pl.multiple_of(k * KT, KT), KT)], zt.at[slot], zt_sem.at[slot])
+        rows = slice(h * HB, (h + 1) * HB)
+        return pltpu.make_async_copy(
+            z_out.at[rows, pl.ds(pl.multiple_of(k * KT, KT), KT)], zt.at[slot, rows], zt_sem.at[2 * h + slot])
 
     def et_load(et, k):
         slot = lax.rem(k, 2)
@@ -385,7 +391,6 @@
             def dzt_store(k, ref):
                 slot = lax.rem(k, 2)
                 return pltpu.make_async_copy(dzt.at[slot], ref.at[pl.ds(pl.multiple_of(lax.rem(k, 4) * KT, KT), KT)], eo_sem.at[slot])
-            acc[...] = jnp.zeros(acc.shape, f32)
             lane = lax.broadcasted_iota(jnp.int32, (PIECE, 128), 1)
 
             def piece(dst, rows, low, k, tie):
@@ -408,7 +413,7 @@
                 for n in range(DIM // NCOL):
                     cols = slice(n * NCOL, (n + 1) * NCOL)
                     prod = jnp.dot(src[...], et[slot, :, cols], preferred_element_type=f32)
-                    acc[base:base + HB, cols] += prod
+                    acc[base:base + HB, cols] = jnp.where(k == 0, 0.0, acc[base:base + HB, cols]) + prod
                     for q in range(0, per, PIECE):
                         at = q * HB // per
                         low = n * per + q
@@ -417,7 +422,7 @@
                         low = n * per
                         dzt[slot, :, base + low:base + low + 256] = jnp.transpose(src[low:low + 256, :])
 
-            z_load(zt, 0).wait()
+            z_load(zt, 0, 0).wait()
 
             def first(i, c):
                 rows = pl.ds(pl.multiple_of(i * PIECE, PIECE), PIECE)
@@ -426,10 +431,15 @@
             lax.fori_loop(0, HB // PIECE, first, 0)
 
             def step(k, c):
+                @pl.when(k + 2 < VOCAB // KT)
+                def _():
+                    z_load(zt, k + 2, 0).start()
+
                 @pl.when(k + 1 < VOCAB // KT)
                 def _():
-                    z_load(zt, k + 1).start()
+                    z_load(zt, k + 1, 1).start()
                     et_load(et, k + 1).start()
+                    z_load(zt, k + 1, 0).wait()
                 for at, j in WAIT_STEP.items():
                     @pl.when(k == at)
                     def _(j=j):
@@ -443,11 +453,8 @@
                 def _():
                     dzt_copy(k - 2).start()
                 et_load(et, k).wait()
+                z_load(zt, k, 1).wait()
                 half_step(k, da, db, 0, HB, k)
-
-                @pl.when(k + 1 < VOCAB // KT)
-                def _():
-                    z_load(zt, k + 1).wait()
                 half_step(k, db, da, HB, 0, k + 1)
 
                 @pl.when(k < 4)
@@ -510,13 +517,19 @@
                             d_bias = d_bias + (dx[0:8] + dx[8:16])
                         gb_v[0, :, cols] = d_gain
                         gb_v[1, :, cols] = d_bias
-                    c1 = [jnp.broadcast_to(jnp.sum(v, axis=-1, keepdims=True) * (1.0 / DIM), (16, 128)) for v in sum1]
-                    c3 = [jnp.broadcast_to(jnp.sum(v, axis=-1, keepdims=True) * (1.0 / DIM), (16, 128)) for v in sum3]
+                    slope, shift = [], []
                     for u in units:
+                        mean, rstd = mr[0, row[u], :], mr[1, row[u], :]
+                        c1 = jnp.broadcast_to(jnp.sum(sum1[u], axis=-1, keepdims=True) * (1.0 / DIM), (16, 128))
+                        c3 = jnp.broadcast_to(jnp.sum(sum3[u], axis=-1, keepdims=True) * (1.0 / DIM), (16, 128))
+                        slope.append(c3 * rstd * rstd)
+                        shift.append(slope[u] * mean - c1 * rstd)
+                    for u in units:
+                        rstd = mr[1, row[u], :]
                         for k in range(DIM // 128):
                             cols = slice(k * 128, (k + 1) * 128)
-                            _, xhat, gx = load(u, cols)
-                            ob[slot, low[u], cols] = (mr[1, row[u], :] * (gx - c1[u] - xhat * c3[u])).astype(jnp.bfloat16)
+                            gx = acc[row[u], cols] * jnp.concatenate([g8[:, cols]] * 2, axis=0)
+                            ob[slot, low[u], cols] = (gx * rstd - hb[slot, low[u], cols].astype(f32) * slope[u] + shift[u]).astype(bf16)
                     return c2
                 lax.fori_loop(0, NB_ROWS // (16 * NB_UNROLL), rows_body, 0)
                 o_store(i).start()
@@ -554,16 +567,16 @@
                     x_load(x_part, (i - 4) * KT, slot).start()
                     dz_load(dzt_part, (i - 4) * KT, slot).start()
 
-            def add(slot):
+            def add(slot, first):
                 def mul(h, c2):
                     rows = pl.ds(pl.multiple_of(h * HB, HB), HB)
                     for n in range(0, DIM, NCOL):
-                        acc[rows, n:n + NCOL] += jnp.dot(dzb[slot, rows, :], xt[slot, :, n:n + NCOL], preferred_element_type=jnp.float32)
+                        prod = jnp.dot(dzb[slot, rows, :], xt[slot, :, n:n + NCOL], preferred_element_type=f32)
+                        acc[rows, n:n + NCOL] = jnp.where(first, 0.0, acc[rows, n:n + NCOL]) + prod
                     return c2
                 lax.fori_loop(0, HBS, mul, 0)
 
             start_local(0)
-            acc[...] = jnp.zeros(acc.shape, f32)
 
             def rem_load(r):
                 slot = lax.rem(r, 2)
@@ -592,7 +605,7 @@
                     for p, dev in group:
                         remote(gs_v, gsum_all.at[tp], g_send, g_recv.at[p], dev).start()
 
-                @pl.when(i == 5)
+                @pl.when(i == 6)
                 def _():
                     xt_event(4)
 
@@ -607,7 +620,7 @@
                         cp.start()
                 x_load(x_out, 0, slot).wait()
                 dz_load(dzt_own, 0, slot).wait()
-                add(slot)
+                add(slot, i == 0)
                 return c
             lax.fori_loop(0, 8, local, 0)
             eo_load.wait()
@@ -741,7 +754,7 @@
         scratch_shapes=[
             pltpu.VMEM((3, GROUPS, 128), i32), pltpu.VMEM((2, GROUPS, 128), f32), pltpu.VMEM(small, f32), pltpu.VMEM(ints, i32),
             pltpu.VMEM((2, 8, DIM), f32), pltpu.VMEM((2, DIM), f32), pltpu.VMEM((8, DIM), f32),
-            dma((2,)), dma, dma((2,)), dma((2,)), dma((2,)), dma((2,)), dma((2,)), dma((2,)), dma((2,)), dma, dma,
+            dma((2,)), dma, dma((2,)), dma((2,)), dma((2,)), dma((4,)), dma((2,)), dma((2,)), dma((2,)), dma, dma,
             dma, dma, dma, dma, dma, dma, dma, dma, dma, dma,
             dma((CHUNKS,)), dma((CHUNKS,)), dma((TILES - NEAR,)), dma((ROWS // PE_ROWS,)), dma((4,)), dma((4,)),
             dma((XCHS,)), dma((XCHS,)), dma, dma((4,)), dma((4,)),

time: 649 us -> 642 us (0.989)
  no operation moved by 1% of the time
where the time goes in v6:
time: 642 us; the launch traced here: 641 us
  Pallas kernels  639 us (100%)
    pallas_call x1, Pallas kernels, run_step(): pl.pallas_call(step_kernel, name='step', out_shape=[jax.ShapeDtypeStruct(...  589 us
    pallas_call x1, Pallas kernels, finish(): pl.pallas_call(finish_kernel, name='finish', grid=(steps,), out_shape=[ja...  49.8 us

profile of v6, /device:TPU:0, one launch (start us, length us, event | category | flops | bytes accessed | tf_op | source)
XLA Modules:
  0.0 641.5 jit_solution(3771041732079555069)
XLA Ops:
  0.6 0.7 fusion.6
  1.4 1.3 pad_add_fusion.info
  2.7 588.8 %step.1 = (bf16[8192,4096]{1,0:T(8,128)(2,1)}, bf16[2048,4096]{1,0:T(8,128)(2,1)}, f32[2048,8192]{1,0:T(8,128)}, f32[4,2,16,128]{3,2,1,0:T(8,128)}, s32[4,3,16,1...) custom-call(bf16[2048,4096]{1,0:T(8,128)(2,1)} %hid.1, ...), custom_call_target="tpu_custom_call" | custom-call | flops 824633720832 | bytes 734003200 | tf_op jit(solution)/shard_map/step/pallas_call | solution.py:748
  591.5 49.8 %finish.1 = (f32[2048,4096]{1,0:T(8,128)}, bf16[2048,4096]{1,0:T(8,128)(2,1)}, f32[16,128]{1,0:T(8,128)}, f32[1,1]{1,0:T(1,128)}, f32[1,4096]{1,0:T(1,128)}, /*index=5*/f32[1,4096]{1,0:T(1,128)}) custom-call(f32[2048,4096]{1,0:T(8,128)} %get-tuple-element.20.refs_0_, bf16[2,2048,1024]{2,1,0:T(8,128)(2,1)} %get-tuple-element.21.refs_1_.refs_2_, ...), custom_call_target="tpu_custom_call" | custom-call | flops 34359738368 | bytes 125829120 | tf_op jit(solution)/shard_map/finish/pallas_call | solution.py:807

commit v7 on v6

--- a/solution.py
+++ b/solution.py
@@ -656,8 +656,7 @@
 
                 @pl.when(r > XCHS - DEFER + 1)
                 def _():
-                    dz_out(0, 0, slot).wait()
-                    dz_out(0, 1, slot).wait()
+                    dz_out(0, slot).wait()
 
                 far_rows = []
                 for g in range(4):
@@ -666,6 +665,9 @@
                     far_rows.append((stats[who, 0, at, :], infos[who, 1, at, :].astype(f32) / count, infos[who, 0, at, :] - tp * ROWS))
 
                 def logits(h, c2):
+                    @pl.when((r == XCHS - 2) & (h == ROWS // ZB // 2))
+                    def _():
+                        xt_event(XCHS - 1)
                     for k in range(0, DIM, KCOL):
                         prod = lax.dot_general(eo[pl.ds(pl.multiple_of(h * ZB, ZB), ZB), k:k + KCOL], xt[slot, :, k:k + KCOL], NT, preferred_element_type=jnp.float32)
                         zs[...] = prod if k == 0 else zs[...] + prod
@@ -680,11 +682,6 @@
                     return c2
                 lax.fori_loop(0, ROWS // ZB, logits, 0)
 
-                @pl.when(r == XCHS - 2)
-                def _():
-                    xt_event(XCHS - 1)
-                    fetch()
-
                 @pl.when(r < XCHS - DEFER)
                 def _():
                     def mul(h, c2):
@@ -696,17 +693,15 @@
 
                 @pl.when(r >= XCHS - DEFER)
                 def _():
-                    for i in range(2):
-                        dz_out(r - (XCHS - DEFER), i, slot).start()
+                    dz_out(r - (XCHS - DEFER), slot).start()
                 return c
 
-            def dz_out(q, i, slot):
-                return pltpu.make_async_copy(
-                    dzb.at[slot, :, pl.ds(i * XCH, XCH)], dzt_last.at[i, :, pl.ds(pl.multiple_of(q * XCH, XCH), XCH)], dzo_sem.at[slot])
-            lax.fori_loop(0, XCHS, far, 0)
+            def dz_out(q, slot):
+                return pltpu.make_async_copy(dzb.at[slot], dzt_last.at[q], dzo_sem.at[slot])
+            lax.fori_loop(0, XCHS - 1, far, 0)
             for slot in range(2):
-                dz_out(0, 0, slot).wait()
-                dz_out(0, 1, slot).wait()
+                dz_out(0, slot).wait()
+            xd_copy(XCHS - 1).wait_recv()
             pltpu.make_async_copy(acc, de_part, big_sem).wait()
         pl.run_scoped(e_phase, pltpu.VMEM((ROWS, DIM), jnp.bfloat16), pltpu.VMEM((2, KT, DIM), jnp.bfloat16),
                       pltpu.VMEM((2, ROWS, KT), jnp.bfloat16), pltpu.VMEM((ZB, KT), jnp.float32))
@@ -744,7 +739,7 @@
     small, ints = (4, 2, GROUPS, 128), (4, 3, GROUPS, 128)
     mat, square = ((TOK, DIM), bf16), ((ROWS, TOK), bf16)
     shapes = [((VOCAB, DIM), bf16), mat, ((TOK, VOCAB), f32), (small, f32), (ints, i32),
-              mat, mat, mat, mat, square, square, square, ((2, ROWS, DEFER * XCH), bf16), ((ROWS, DIM), f32), ((4, 2, DIM), f32)]
+              mat, mat, mat, mat, square, square, square, ((DEFER - 1, ROWS, KT), bf16), ((ROWS, DIM), f32), ((4, 2, DIM), f32)]
     return pl.pallas_call(
         step_kernel,
         name="step",
@@ -764,64 +759,158 @@
     )(hidden, gain, bias, embed, info)
 
 
-def finish_kernel(*refs):
-    nb = DEFER * XCH // KT
-    de_in, dz0, dz1 = refs[:3]
-    xs = refs[3:3 + 2 * nb]
-    dh_in, stat_all, info_all, gsum_all, de_out, dh_out, loss, mean, d_gain, d_bias = refs[3 + 2 * nb:]
-    for h in range(HBS):
-        rows = slice(h * HB, (h + 1) * HB)
-        prod = None
-        for b in range(nb):
-            for dz, x in ((dz0, xs[b]), (dz1, xs[nb + b])):
-                part = jnp.dot(dz[0, rows, b * KT:(b + 1) * KT], x[...], preferred_element_type=jnp.float32)
+def finish_kernel(de_in, dzt_last, x_xp, x_xq, emb, dh_in, stat_all, info_all, gsum_all,
+                  de_out, dh_out, loss, mean, d_gain, d_bias,
+                  xr, dz, eb, zs, din, dout, hb, x_sem, z_sem, e_sem, di_sem, do_sem, hi_sem, ho_sem):
+    f32, bf16 = jnp.float32, jnp.bfloat16
+    last = DEFER - 1
+
+    def x_loads(q):
+        rows = pl.ds((XCHS - DEFER + q) * XCH, XCH)
+        return [pltpu.make_async_copy(ref.at[rows], xr.at[q, pl.ds(i * XCH, XCH)], x_sem.at[q]) for i, ref in enumerate((x_xp, x_xq))]
+
+    def x_wait(q):
+        pltpu.make_async_copy(xr.at[q], xr.at[q], x_sem.at[q]).wait()
+
+    def e_load(h):
+        slot = lax.rem(h, 2)
+        return pltpu.make_async_copy(emb.at[pl.ds(pl.multiple_of(h * ZB, ZB), ZB)], eb.at[slot], e_sem.at[slot])
+
+    def z_load(q):
+        return pltpu.make_async_copy(dzt_last.at[q], dz.at[q], z_sem.at[q])
+
+    def tile(ref, i):
+        return ref.at[:, pl.ds(pl.multiple_of(i * KT, KT), KT)]
+
+    def d_load(i):
+        slot = lax.rem(i, 2)
+        return pltpu.make_async_copy(tile(de_in, i), din.at[slot], di_sem.at[slot])
+
+    def d_store(i):
+        slot = lax.rem(i, 2)
+        return pltpu.make_async_copy(dout.at[slot], tile(de_out, i), do_sem.at[slot])
+    steps = DIM // KT
+    per = TOK // steps
+
+    def h_load(i):
+        slot = lax.rem(i, 2)
+        return pltpu.make_async_copy(dh_in.at[pl.ds(pl.multiple_of(i * per, per), per)], hb.at[slot], hi_sem.at[slot])
+
+    def h_store(i):
+        slot = lax.rem(i, 2)
+        return pltpu.make_async_copy(hb.at[slot], dh_out.at[pl.ds(pl.multiple_of(i * per, per), per)], ho_sem.at[slot])
+    for cp in x_loads(last):
+        cp.start()
+    e_load(0).start()
+    e_load(1).start()
+    for q in range(last):
+        z_load(q).start()
+        for cp in x_loads(q):
+            cp.start()
+    d_load(0).start()
+    h_load(0).start()
+    d_load(1).start()
+
+    tp = lax.axis_index('tp')
+    core = lax.rem(tp, 2)
+    other = 2 - (tp - core)
+    weights = info_all[:, 1].astype(f32)
+    total = jnp.sum(weights)
+    all_loss = (stat_all[:, 0] - stat_all[:, 1]) * weights
+    loss[...] = (stat_all[tp, 0] - stat_all[tp, 1]) * info_all[tp, 1].astype(f32)
+    mean[...] = jnp.broadcast_to(jnp.sum(all_loss), (1, 1)) / jnp.broadcast_to(total, (1, 1))
+    sums = ((gsum_all[0] + gsum_all[1]) + gsum_all[2]) + gsum_all[3]
+    d_gain[...] = sums[0:1]
+    d_bias[...] = sums[1:2]
+    count = jnp.broadcast_to(total, (1, 128))
+    far_rows = []
+    for g in range(4):
+        who = other + core if g < 2 else other + 1 - core
+        at = slice(GROUPS - 2 + g % 2, GROUPS - 1 + g % 2)
+        far_rows.append((stat_all[who, 0, at, :], info_all[who, 1, at, :].astype(f32) / count, info_all[who, 0, at, :] - tp * ROWS))
+    x_wait(last)
+
+    def logits(h, c):
+        slot = lax.rem(h, 2)
+        e_load(h).wait()
+        for k in range(0, DIM, KCOL):
+            prod = lax.dot_general(eb[slot, :, k:k + KCOL], xr[last, :, k:k + KCOL], NT, preferred_element_type=f32)
+            zs[...] = prod if k == 0 else zs[...] + prod
+
+        @pl.when(h + 2 < ROWS // ZB)
+        def _():
+            e_load(h + 2).start()
+        for q in range(ZB // 32):
+            row = h * ZB + q * 32
+            line = lax.broadcasted_iota(jnp.int32, (32, 128), 0)
+            for g, (lse, scale, trel) in enumerate(far_rows):
+                cols = slice(g * 128, (g + 1) * 128)
+                hot = ((trel - row) == line).astype(f32)
+                val = (jnp.exp(zs[q * 32:(q + 1) * 32, cols] - lse) - hot) * scale
+                dz[last, pl.ds(pl.multiple_of(row, 32), 32), cols] = val.astype(bf16)
+        return c
+    lax.fori_loop(0, ROWS // ZB, logits, 0)
+    for q in range(last):
+        z_load(q).wait()
+        x_wait(q)
+
+    def step(i, c):
+        slot = lax.rem(i, 2)
+        cols = pl.ds(pl.multiple_of(i * KT, KT), KT)
+        d_load(i).wait()
+        h_load(i).wait()
+        h_store(i).start()
+
+        @pl.when(i >= 1)
+        def _():
+            h_store(i - 1).wait()
+
+        @pl.when(i + 1 < steps)
+        def _():
+            h_load(i + 1).start()
+
+        @pl.when(i >= 2)
+        def _():
+            d_store(i - 2).wait()
+        for h in range(HBS):
+            rows = slice(h * HB, (h + 1) * HB)
+            prod = None
+            for q in range(DEFER):
+                part = jnp.dot(dz[q, rows, :], xr[q, :, cols], preferred_element_type=f32)
                 prod = part if prod is None else prod + part
-        de_out[rows, :] = de_in[rows, :] + prod
-    dh_out[...] = dh_in[...]
-
-    @pl.when(pl.program_id(0) == 0)
-    def _():
-        weights = info_all[:, 1].astype(jnp.float32)
-        all_loss = (stat_all[:, 0] - stat_all[:, 1]) * weights
-        tp = lax.axis_index('tp')
-        loss[...] = (stat_all[tp, 0] - stat_all[tp, 1]) * info_all[tp, 1].astype(jnp.float32)
-        mean[...] = jnp.broadcast_to(jnp.sum(all_loss), (1, 1)) / jnp.broadcast_to(jnp.sum(weights), (1, 1))
-        sums = ((gsum_all[0] + gsum_all[1]) + gsum_all[2]) + gsum_all[3]
-        d_gain[...] = sums[0:1]
-        d_bias[...] = sums[1:2]
-
-
-def finish(de_part, dzt_last, x_xp, x_xq, dhid, stat_all, info_all, gsum_all):
-    cols = 512
-    steps = DIM // cols
-    depth = DEFER * XCH
-    rows = TOK // steps
-    first = (TOK - depth) // KT
-    once = pl.Buffered(1)
-    x_specs = [pl.BlockSpec((KT, cols), lambda i, b=b: (b, i)) for b in range(first, TOK // KT)]
-
-    def whole(shape):
-        return pl.BlockSpec(shape, lambda i: (0,) * len(shape))
-    nb = len(x_specs)
-    outs = [((ROWS, DIM), jnp.float32), ((TOK, DIM), jnp.bfloat16), ((GROUPS, 128), jnp.float32), ((1, 1), jnp.float32), ((1, DIM), jnp.float32), ((1, DIM), jnp.float32)]
+            dout[slot, rows, :] = din[slot, rows, :] + prod
+        d_store(i).start()
+
+        @pl.when(i + 2 < steps)
+        def _():
+            d_load(i + 2).start()
+        return c
+    lax.fori_loop(0, steps, step, 0)
+    d_store(steps - 2).wait()
+    d_store(steps - 1).wait()
+    h_store(steps - 1).wait()
+
+
+def finish(de_part, dzt_last, x_xp, x_xq, embed, dhid, stat_all, info_all, gsum_all):
+    any_spec = pl.BlockSpec(memory_space=pl.ANY)
+    vmem_spec = pl.BlockSpec(memory_space=pltpu.VMEM)
+    f32, bf16 = jnp.float32, jnp.bfloat16
+    dma = pltpu.SemaphoreType.DMA
+    outs = [((ROWS, DIM), f32), ((TOK, DIM), bf16), ((GROUPS, 128), f32), ((1, 1), f32), ((1, DIM), f32), ((1, DIM), f32)]
     return pl.pallas_call(
         finish_kernel,
         name="finish",
-        grid=(steps,),
         out_shape=[jax.ShapeDtypeStruct(s, d) for s, d in outs],
-        in_specs=[
-            pl.BlockSpec((ROWS, cols), lambda i: (0, i)),
-            pl.BlockSpec((1, ROWS, depth), lambda i: (0, 0, 0), pipeline_mode=once),
-            pl.BlockSpec((1, ROWS, depth), lambda i: (1, 0, 0), pipeline_mode=once),
-            *x_specs, *x_specs,
-            pl.BlockSpec((rows, DIM), lambda i: (i, 0)),
-            whole(stat_all.shape), whole(info_all.shape), whole(gsum_all.shape),
+        in_specs=[any_spec] * 6 + [vmem_spec] * 3,
+        out_specs=[any_spec] * 2 + [vmem_spec] * 4,
+        scratch_shapes=[
+            pltpu.VMEM((DEFER, KT, DIM), bf16), pltpu.VMEM((DEFER, ROWS, KT), bf16), pltpu.VMEM((2, ZB, DIM), bf16), pltpu.VMEM((ZB, KT), f32),
+            pltpu.VMEM((2, ROWS, KT), f32), pltpu.VMEM((2, ROWS, KT), f32), pltpu.VMEM((2, TOK // (DIM // KT), DIM), bf16),
+            dma((DEFER,)), dma((DEFER,)), dma((2,)), dma((2,)), dma((2,)), dma((2,)), dma((2,)),
         ],
-        out_specs=[pl.BlockSpec((ROWS, cols), lambda i: (0, i)), pl.BlockSpec((rows, DIM), lambda i: (i, 0)),
-                   whole((GROUPS, 128)), whole((1, 1)), whole((1, DIM)), whole((1, DIM))],
-        compiler_params=pltpu.CompilerParams(vmem_limit_bytes=60 * 1024 * 1024),
-        cost_estimate=pl.CostEstimate(flops=4 * ROWS * DIM * depth, bytes_accessed=120 * 2 ** 20, transcendentals=0),
-    )(de_part, dzt_last, dzt_last, *[x_xp] * nb, *[x_xq] * nb, dhid, stat_all, info_all, gsum_all)
+        compiler_params=pltpu.CompilerParams(vmem_limit_bytes=67043328),
+        cost_estimate=pl.CostEstimate(flops=2 * ROWS * DIM * KT * (DEFER + 1), bytes_accessed=130 * 2 ** 20, transcendentals=ROWS * KT),
+    )(de_part, dzt_last, x_xp, x_xq, embed, dhid, stat_all, info_all, gsum_all)
 
 
 def solution(mesh):
@@ -838,7 +927,7 @@
         info = jnp.stack([targets, loss_mask, tcol]).reshape(3, GROUPS, 128)
         outs = run_step(hidden, ln_gain.reshape(1, DIM), ln_bias.reshape(1, DIM), embed, info)
         stat_all, info_all, dhid, x_xp, x_xq, dzt_last, de_part, gsum_all = (outs[i] for i in (3, 4, 5, 7, 8, 12, 13, 14))
-        d_embed, d_hidden, loss, mean, d_gain, d_bias = finish(de_part, dzt_last, x_xp, x_xq, dhid, stat_all, info_all, gsum_all)
+        d_embed, d_hidden, loss, mean, d_gain, d_bias = finish(de_part, dzt_last, x_xp, x_xq, embed, dhid, stat_all, info_all, gsum_all)
         return loss.reshape(TOK), mean.reshape(1), d_hidden, d_embed, d_gain.reshape(DIM), d_bias.reshape(DIM)
 
     token_rows = P(('dp', 'tp'))

time: 642 us -> 637 us (level)
    pallas_call x1, Pallas kernels: 589 us -> 573 us  [run_step(): pl.pallas_call(step_kernel, name='step', out_shape=[jax.ShapeDtypeStruct(...]
    pallas_call x1, Pallas kernels: 49.8 us -> 60.8 us  [finish(): pl.pallas_call(finish_kernel, name='finish', out_shape=[jax.ShapeDtypeStr...]
where the time goes in v7:
time: 637 us; the launch traced here: 636 us
  Pallas kernels  633 us (99%)
    pallas_call x1, Pallas kernels, run_step(): pl.pallas_call(step_kernel, name='step', out_shape=[jax.ShapeDtypeStruct(...  573 us
    pallas_call x1, Pallas kernels, finish(): pl.pallas_call(finish_kernel, name='finish', out_shape=[jax.ShapeDtypeStr...  60.8 us

profile of v7, /device:TPU:0, one launch (start us, length us, event | category | flops | bytes accessed | tf_op | source)
XLA Modules:
  0.0 636.2 jit_solution(6521531425168478043)
XLA Ops:
  0.6 0.7 fusion.6
  1.4 1.3 pad_add_fusion.info
  2.7 572.5 %step.1 = (bf16[8192,4096]{1,0:T(8,128)(2,1)}, bf16[2048,4096]{1,0:T(8,128)(2,1)}, f32[2048,8192]{1,0:T(8,128)}, f32[4,2,16,128]{3,2,1,0:T(8,128)}, s32[4,3,16,1...) custom-call(bf16[2048,4096]{1,0:T(8,128)(2,1)} %hid.1, ...), custom_call_target="tpu_custom_call" | custom-call | flops 824633720832 | bytes 734003200 | tf_op jit(solution)/shard_map/step/pallas_call | solution.py:743
  575.2 60.8 %finish.1 = (f32[2048,4096]{1,0:T(8,128)}, bf16[2048,4096]{1,0:T(8,128)(2,1)}, f32[16,128]{1,0:T(8,128)}, f32[1,1]{1,0:T(1,128)}, f32[1,4096]{1,0:T(1,128)}, /*index=5*/f32[1,4096]{1,0:T(1,128)}) custom-call(f32[2048,4096]{1,0:T(8,128)} %get-tuple-element.20.de_in, bf16[3,2048,512]{2,1,0:T(8,128)(2,1)} %get-tuple-element.21.dzt_last, ...), custom_call_target="tpu_custom_call" | custom-call | flops 42949672960 | bytes 136314880 | tf_op jit(solution)/shard_map/finish/pallas_call | solution.py:900

commit v8 on v7

--- a/solution.py
+++ b/solution.py
@@ -761,16 +761,19 @@
 
 def finish_kernel(de_in, dzt_last, x_xp, x_xq, emb, dh_in, stat_all, info_all, gsum_all,
                   de_out, dh_out, loss, mean, d_gain, d_bias,
-                  xr, dz, eb, zs, din, dout, hb, x_sem, z_sem, e_sem, di_sem, do_sem, hi_sem, ho_sem):
+                  x7, xr, dz, eb, zs, din, dout, hb, x_sem, z_sem, e_sem, di_sem, do_sem, hi_sem, ho_sem):
     f32, bf16 = jnp.float32, jnp.bfloat16
     last = DEFER - 1
 
-    def x_loads(q):
-        rows = pl.ds((XCHS - DEFER + q) * XCH, XCH)
-        return [pltpu.make_async_copy(ref.at[rows], xr.at[q, pl.ds(i * XCH, XCH)], x_sem.at[q]) for i, ref in enumerate((x_xp, x_xq))]
-
-    def x_wait(q):
-        pltpu.make_async_copy(xr.at[q], xr.at[q], x_sem.at[q]).wait()
+    def x_last():
+        rows = pl.ds((XCHS - 1) * XCH, XCH)
+        return [pltpu.make_async_copy(ref.at[rows], x7.at[pl.ds(i * XCH, XCH)], x_sem.at[3]) for i, ref in enumerate((x_xp, x_xq))]
+
+    def x_tiles(i):
+        slot = lax.rem(i, 3)
+        cols = pl.ds(pl.multiple_of(i * KT, KT), KT)
+        rows = pl.ds((XCHS - DEFER) * XCH, last * XCH)
+        return [pltpu.make_async_copy(ref.at[rows, cols], xr.at[slot, j], x_sem.at[slot]) for j, ref in enumerate((x_xp, x_xq))]
 
     def e_load(h):
         slot = lax.rem(h, 2)
@@ -783,11 +786,11 @@
         return ref.at[:, pl.ds(pl.multiple_of(i * KT, KT), KT)]
 
     def d_load(i):
-        slot = lax.rem(i, 2)
+        slot = lax.rem(i, 3)
         return pltpu.make_async_copy(tile(de_in, i), din.at[slot], di_sem.at[slot])
 
     def d_store(i):
-        slot = lax.rem(i, 2)
+        slot = lax.rem(i, 3)
         return pltpu.make_async_copy(dout.at[slot], tile(de_out, i), do_sem.at[slot])
     steps = DIM // KT
     per = TOK // steps
@@ -799,17 +802,14 @@
     def h_store(i):
         slot = lax.rem(i, 2)
         return pltpu.make_async_copy(hb.at[slot], dh_out.at[pl.ds(pl.multiple_of(i * per, per), per)], ho_sem.at[slot])
-    for cp in x_loads(last):
+    for cp in x_last():
         cp.start()
     e_load(0).start()
     e_load(1).start()
-    for q in range(last):
-        z_load(q).start()
-        for cp in x_loads(q):
+
+    def tile_loads(i):
+        for cp in (*x_tiles(i), d_load(i)):
             cp.start()
-    d_load(0).start()
-    h_load(0).start()
-    d_load(1).start()
 
     tp = lax.axis_index('tp')
     core = lax.rem(tp, 2)
@@ -828,18 +828,34 @@
         who = other + core if g < 2 else other + 1 - core
         at = slice(GROUPS - 2 + g % 2, GROUPS - 1 + g % 2)
         far_rows.append((stat_all[who, 0, at, :], info_all[who, 1, at, :].astype(f32) / count, info_all[who, 0, at, :] - tp * ROWS))
-    x_wait(last)
+    pltpu.make_async_copy(x7, x7, x_sem.at[3]).wait()
 
     def logits(h, c):
         slot = lax.rem(h, 2)
         e_load(h).wait()
         for k in range(0, DIM, KCOL):
-            prod = lax.dot_general(eb[slot, :, k:k + KCOL], xr[last, :, k:k + KCOL], NT, preferred_element_type=f32)
+            prod = lax.dot_general(eb[slot, :, k:k + KCOL], x7[:, k:k + KCOL], NT, preferred_element_type=f32)
             zs[...] = prod if k == 0 else zs[...] + prod
 
-        @pl.when(h + 2 < ROWS // ZB)
+        @pl.when(h == 0)
         def _():
-            e_load(h + 2).start()
+            e_load(2).start()
+            z_load(0).start()
+            z_load(1).start()
+
+        @pl.when(h == 1)
+        def _():
+            e_load(3).start()
+            z_load(2).start()
+
+        @pl.when(h == 2)
+        def _():
+            tile_loads(0)
+            h_load(0).start()
+
+        @pl.when(h == 3)
+        def _():
+            tile_loads(1)
         for q in range(ZB // 32):
             row = h * ZB + q * 32
             line = lax.broadcasted_iota(jnp.int32, (32, 128), 0)
@@ -852,12 +868,14 @@
     lax.fori_loop(0, ROWS // ZB, logits, 0)
     for q in range(last):
         z_load(q).wait()
-        x_wait(q)
 
     def step(i, c):
-        slot = lax.rem(i, 2)
+        slot = lax.rem(i, 3)
         cols = pl.ds(pl.multiple_of(i * KT, KT), KT)
-        d_load(i).wait()
+
+        @pl.when(i + 2 < steps)
+        def _():
+            tile_loads(i + 2)
         h_load(i).wait()
         h_store(i).start()
 
@@ -869,25 +887,24 @@
         def _():
             h_load(i + 1).start()
 
-        @pl.when(i >= 2)
+        @pl.when(i >= 3)
         def _():
-            d_store(i - 2).wait()
+            d_store(i - 3).wait()
+        d_load(i).wait()
+        for cp in x_tiles(i):
+            cp.wait()
         for h in range(HBS):
             rows = slice(h * HB, (h + 1) * HB)
-            prod = None
-            for q in range(DEFER):
-                part = jnp.dot(dz[q, rows, :], xr[q, :, cols], preferred_element_type=f32)
-                prod = part if prod is None else prod + part
+            prod = jnp.dot(dz[last, rows, :], x7[:, cols], preferred_element_type=f32)
+            for q in range(last):
+                for j in range(2):
+                    prod = prod + jnp.dot(dz[q, rows, j * XCH:(j + 1) * XCH], xr[slot, j, q * XCH:(q + 1) * XCH, :], preferred_element_type=f32)
             dout[slot, rows, :] = din[slot, rows, :] + prod
         d_store(i).start()
-
-        @pl.when(i + 2 < steps)
-        def _():
-            d_load(i + 2).start()
         return c
     lax.fori_loop(0, steps, step, 0)
-    d_store(steps - 2).wait()
-    d_store(steps - 1).wait()
+    for i in range(3):
+        d_store(steps - 3 + i).wait()
     h_store(steps - 1).wait()
 
 
@@ -904,9 +921,9 @@
         in_specs=[any_spec] * 6 + [vmem_spec] * 3,
         out_specs=[any_spec] * 2 + [vmem_spec] * 4,
         scratch_shapes=[
-            pltpu.VMEM((DEFER, KT, DIM), bf16), pltpu.VMEM((DEFER, ROWS, KT), bf16), pltpu.VMEM((2, ZB, DIM), bf16), pltpu.VMEM((ZB, KT), f32),
-            pltpu.VMEM((2, ROWS, KT), f32), pltpu.VMEM((2, ROWS, KT), f32), pltpu.VMEM((2, TOK // (DIM // KT), DIM), bf16),
-            dma((DEFER,)), dma((DEFER,)), dma((2,)), dma((2,)), dma((2,)), dma((2,)), dma((2,)),
+            pltpu.VMEM((KT, DIM), bf16), pltpu.VMEM((3, 2, (DEFER - 1) * XCH, KT), bf16), pltpu.VMEM((DEFER, ROWS, KT), bf16), pltpu.VMEM((2, ZB, DIM), bf16), pltpu.VMEM((ZB, KT), f32),
+            pltpu.VMEM((3, ROWS, KT), f32), pltpu.VMEM((3, ROWS, KT), f32), pltpu.VMEM((2, TOK // (DIM // KT), DIM), bf16),
+            dma((4,)), dma((DEFER,)), dma((2,)), dma((3,)), dma((3,)), dma((2,)), dma((2,)),
         ],
         compiler_params=pltpu.CompilerParams(vmem_limit_bytes=67043328),
         cost_estimate=pl.CostEstimate(flops=2 * ROWS * DIM * KT * (DEFER + 1), bytes_accessed=130 * 2 ** 20, transcendentals=ROWS * KT),

time: 637 us -> 633 us (level)
  no operation moved by 1% of the time
where the time goes in v8:
time: 633 us
  Pallas kernels  630 us (100%)
    pallas_call x1, Pallas kernels, run_step(): pl.pallas_call(step_kernel, name='step', out_shape=[jax.ShapeDtypeStruct(...  573 us
    pallas_call x1, Pallas kernels, finish(): pl.pallas_call(finish_kernel, name='finish', out_shape=[jax.ShapeDtypeStr...  57.1 us

profile of v8, /device:TPU:0, one launch (start us, length us, event | category | flops | bytes accessed | tf_op | source)
XLA Modules:
  0.0 632.5 jit_solution(1893716688548434553)
XLA Ops:
  0.6 0.7 fusion.6
  1.4 1.3 pad_add_fusion.info
  2.7 572.5 %step.1 = (bf16[8192,4096]{1,0:T(8,128)(2,1)}, bf16[2048,4096]{1,0:T(8,128)(2,1)}, f32[2048,8192]{1,0:T(8,128)}, f32[4,2,16,128]{3,2,1,0:T(8,128)}, s32[4,3,16,1...) custom-call(bf16[2048,4096]{1,0:T(8,128)(2,1)} %hid.1, ...), custom_call_target="tpu_custom_call" | custom-call | flops 824633720832 | bytes 734003200 | tf_op jit(solution)/shard_map/step/pallas_call | solution.py:743
  575.2 57.1 %finish.1 = (f32[2048,4096]{1,0:T(8,128)}, bf16[2048,4096]{1,0:T(8,128)(2,1)}, f32[16,128]{1,0:T(8,128)}, f32[1,1]{1,0:T(1,128)}, f32[1,4096]{1,0:T(1,128)}, /*index=5*/f32[1,4096]{1,0:T(1,128)}) custom-call(f32[2048,4096]{1,0:T(8,128)} %get-tuple-element.20.de_in, bf16[3,2048,512]{2,1,0:T(8,128)(2,1)} %get-tuple-element.21.dzt_last, ...), custom_call_target="tpu_custom_call" | custom-call | flops 42949672960 | bytes 136314880 | tf_op jit(solution)/shard_map/finish/pallas_call | solution.py:917

commit v9 on v8

--- a/solution.py
+++ b/solution.py
@@ -59,10 +59,10 @@
     dst[rows, :] = jnp.transpose(jnp.broadcast_to(row, (128, 128)))
 
 
-def step_kernel(hid, gain, bias, emb, info,
+def step_kernel(hid, gain, bias, emb, targets, mask,
                 e_all, x_out, z_out, stat_all, info_all,
                 dhid, x_part, x_xp, x_xq, dzt_own, dzt_out, dzt_part, dzt_last, de_part, gsum_all,
-                info_v, stat_v, stats, infos, gb_v, gs_v, g8,
+                tcol, stat_v, stats, infos, gb_v, gs_v, g8,
                 h_sem, xo_sem, e_sem, eo_sem, z_sem, zt_sem, et_sem, small_sem, dzo_sem, big_sem, g_sem,
                 xs_send, ys_send, ds_send, pe_send, sm_send, xt_send, xd_send, xp_send, dz_send, g_send,
                 x_recv, y_recv, d_recv, pe_recv, info_recv, stat_recv, xt_recv, xd_recv, xp_recv, dz_recv, g_recv):
@@ -77,6 +77,26 @@
         pl.semaphore_signal(barrier, inc=1, device_id=dev, device_id_type=pl.DeviceIdType.MESH)
     pl.semaphore_wait(barrier, 4)
 
+    def info_copies():
+        return [remote(ref, info_all.at[tp, i], sm_send, info_recv.at[2 * p + i], dev)
+                for p, dev in group for i, ref in enumerate((targets, mask))]
+
+    def columns():
+        for s in range(4):
+            pair, odd = s - s % 2, s % 2
+            near = ((tp - core) == pair).astype(jnp.int32)
+            same = (core == odd).astype(jnp.int32)
+            row = targets[...] - s * ROWS
+            low = (row < ROWS // 2).astype(jnp.int32)
+            sub = row - (1 - low) * (ROWS // 2)
+            crossed = low * dp + (1 - low) * (1 - dp)
+            piece = (1 - same) * 2 + crossed
+            tile = (sub.astype(f32) * (1.0 / PIECE_ROWS)).astype(jnp.int32)
+            far = 2 * ROWS + tile * (TILE - PIECE_ROWS) + sub + piece * PIECE_ROWS
+            col = near * ((1 - same) * ROWS + row) + (1 - near) * far
+            inside = (row >= 0) & (row < ROWS)
+            tcol[...] = jnp.where(inside, col, 0 if s == 0 else tcol[...])
+
     def xrows(ref, j):
         return ref.at[pl.ds(pl.multiple_of(j * XCH, XCH), XCH)]
 
@@ -112,15 +132,13 @@
             return remote(emb.at[pl.ds(pl.multiple_of(i * PE_ROWS, PE_ROWS), PE_ROWS)],
                           e_all.at[pl.ds(pl.multiple_of(ROWS + i * PE_ROWS, PE_ROWS), PE_ROWS)], pe_send, pe_recv.at[i], part)
 
-        cp = pltpu.make_async_copy(info, info_v, small_sem.at[0])
-        cp.start()
 
         def h_copy(i):
             return pltpu.make_async_copy(hid.at[pl.ds(pl.multiple_of(i * LN_ROWS, LN_ROWS), LN_ROWS)], hbuf.at[lax.rem(i, 2)], h_sem.at[lax.rem(i, 2)])
         h_copy(0).start()
 
-        for p, dev in group:
-            remote(info, info_all.at[tp], sm_send, info_recv.at[p], dev).start()
+        for cp in info_copies():
+            cp.start()
 
         def start_x(j, c):
             x_copy(j).start()
@@ -155,8 +173,10 @@
             pltpu.make_async_copy(rows, rows, d_recv.at[k]).wait()
             e_load(NEAR + k).start()
 
-        cp.wait()
-        pltpu.make_async_copy(info_v, info_all.at[tp], small_sem.at[0]).start()
+        own_info = [pltpu.make_async_copy(ref, info_all.at[tp, i], small_sem.at[0]) for i, ref in enumerate((targets, mask))]
+        for cp in own_info:
+            cp.start()
+        columns()
         gb8[0] = jnp.broadcast_to(gain[...], (8, DIM))
         gb8[1] = jnp.broadcast_to(bias[...], (8, DIM))
 
@@ -213,7 +233,7 @@
         s_s[...] = jnp.zeros((TOK, 128), jnp.float32)
         t_s[...] = jnp.zeros((TOK, 128), jnp.float32)
         for r in range(GROUPS):
-            spread(info_v[2, r:r + 1, :], slice(r * 128, (r + 1) * 128), tc_v)
+            spread(tcol[r:r + 1, :], slice(r * 128, (r + 1) * 128), tc_v)
         z1[...] = jnp.full((HB, TILE), LOWEST, jnp.float32)
 
         zs = (z0, z1)
@@ -302,15 +322,16 @@
 
             @pl.when(t == NEAR + 1)
             def _():
-                for p, dev in group:
-                    remote(info, info_all.at[tp], sm_send, info_recv.at[p], dev).wait_recv()
-                pltpu.make_async_copy(info_v, info_all.at[tp], small_sem.at[0]).wait()
+                for cp in info_copies():
+                    cp.wait_recv()
+                for cp in own_info:
+                    cp.wait()
                 load = pltpu.make_async_copy(info_all, infos, small_sem.at[0])
                 load.start()
                 load.wait()
                 count = jnp.broadcast_to(token_count(), (1, 128))
                 for r in range(GROUPS):
-                    spread(info_v[1, r:r + 1, :].astype(f32) / count, slice(r * 128, (r + 1) * 128), scale_v)
+                    spread(mask[r:r + 1, :].astype(f32) / count, slice(r * 128, (r + 1) * 128), scale_v)
 
         def step(t, c):
             @pl.when(t > 0)
@@ -338,8 +359,8 @@
         statistics(last, 1)
 
         def finish(i, c):
-            for u in range(4):
-                r = i * 4 + u
+            for u in range(8):
+                r = i * 8 + u
                 rows = pl.ds(pl.multiple_of(r * 128, 128), 128)
                 m = m_s[rows, :]
                 top = jnp.max(m, axis=-1, keepdims=True)
@@ -350,7 +371,7 @@
                 stat_v[0, pl.ds(r, 1), :] = jnp.transpose(lse)[0:1, :]
                 stat_v[1, pl.ds(r, 1), :] = jnp.transpose(tgt)[0:1, :]
             return c
-        lax.fori_loop(0, TOK // 512, finish, 0)
+        lax.fori_loop(0, TOK // 1024, finish, 0)
         for h in range(2):
             z_copy(last, h).wait()
         half = e_all.at[pl.ds(0, ROWS // 2)]
@@ -545,7 +566,7 @@
         own = pltpu.make_async_copy(gs_v, gsum_all.at[tp], g_sem)
         xt_event(3)
 
-        def e_phase(eo, xt, dzb, zs):
+        def e_phase(eo, xt, dzb, zs, z1):
             eo_load = pltpu.make_async_copy(emb, eo, big_sem)
 
             def x_load(ref, row, slot):
@@ -664,23 +685,31 @@
                     at = pl.ds(2 * r + g % 2, 1)
                     far_rows.append((stats[who, 0, at, :], infos[who, 1, at, :].astype(f32) / count, infos[who, 0, at, :] - tp * ROWS))
 
-                def logits(h, c2):
-                    @pl.when((r == XCHS - 2) & (h == ROWS // ZB // 2))
+                def logits(h2, c2):
+                    @pl.when((r == XCHS - 2) & (h2 == 1))
                     def _():
                         xt_event(XCHS - 1)
-                    for k in range(0, DIM, KCOL):
-                        prod = lax.dot_general(eo[pl.ds(pl.multiple_of(h * ZB, ZB), ZB), k:k + KCOL], xt[slot, :, k:k + KCOL], NT, preferred_element_type=jnp.float32)
-                        zs[...] = prod if k == 0 else zs[...] + prod
-                    for q in range(ZB // 32):
-                        row = h * ZB + q * 32
-                        line = lax.broadcasted_iota(jnp.int32, (32, 128), 0)
-                        for g, (lse, scale, trel) in enumerate(far_rows):
-                            cols = slice(g * 128, (g + 1) * 128)
-                            hot = ((trel - row) == line).astype(f32)
-                            val = (jnp.exp(zs[q * 32:(q + 1) * 32, cols] - lse) - hot) * scale
-                            dzb[slot, pl.ds(pl.multiple_of(row, 32), 32), cols] = val.astype(bf16)
+
+                    def multiply(h, z):
+                        for k in range(0, DIM, KCOL):
+                            prod = lax.dot_general(eo[pl.ds(pl.multiple_of(h * ZB, ZB), ZB), k:k + KCOL], xt[slot, :, k:k + KCOL], NT, preferred_element_type=f32)
+                            z[...] = prod if k == 0 else z[...] + prod
+
+                    def convert(h, z):
+                        for q in range(ZB // 32):
+                            row = h * ZB + q * 32
+                            line = lax.broadcasted_iota(jnp.int32, (32, 128), 0)
+                            for g, (lse, scale, trel) in enumerate(far_rows):
+                                cols = slice(g * 128, (g + 1) * 128)
+                                hot = ((trel - row) == line).astype(f32)
+                                val = (jnp.exp(z[q * 32:(q + 1) * 32, cols] - lse) - hot) * scale
+                                dzb[slot, pl.ds(pl.multiple_of(row, 32), 32), cols] = val.astype(bf16)
+                    multiply(2 * h2, zs)
+                    multiply(2 * h2 + 1, z1)
+                    convert(2 * h2, zs)
+                    convert(2 * h2 + 1, z1)
                     return c2
-                lax.fori_loop(0, ROWS // ZB, logits, 0)
+                lax.fori_loop(0, ROWS // (2 * ZB), logits, 0)
 
                 @pl.when(r < XCHS - DEFER)
                 def _():
@@ -704,7 +733,7 @@
             xd_copy(XCHS - 1).wait_recv()
             pltpu.make_async_copy(acc, de_part, big_sem).wait()
         pl.run_scoped(e_phase, pltpu.VMEM((ROWS, DIM), jnp.bfloat16), pltpu.VMEM((2, KT, DIM), jnp.bfloat16),
-                      pltpu.VMEM((2, ROWS, KT), jnp.bfloat16), pltpu.VMEM((ZB, KT), jnp.float32))
+                      pltpu.VMEM((2, ROWS, KT), jnp.bfloat16), pltpu.VMEM((ZB, KT), f32), pltpu.VMEM((ZB, KT), f32))
 
         own.wait()
 
@@ -725,18 +754,19 @@
     pltpu.make_async_copy(x_out, x_out, xd_send).wait()
     xp_copy.wait_send()
     pltpu.make_async_copy(dzt_out, dzt_out, dz_send).wait()
+    for cp in info_copies():
+        cp.wait_send()
     for p, dev in group:
-        remote(info, info_all.at[tp], sm_send, info_recv.at[p], dev).wait_send()
         remote(stat_v, stat_all.at[tp], sm_send, stat_recv.at[p], dev).wait_send()
         remote(gs_v, gsum_all.at[tp], g_send, g_recv.at[p], dev).wait()
 
 
-def run_step(hidden, gain, bias, embed, info):
+def run_step(hidden, gain, bias, embed, targets, mask):
     any_spec = pl.BlockSpec(memory_space=pl.ANY)
     vmem_spec = pl.BlockSpec(memory_space=pltpu.VMEM)
     f32, bf16, i32 = jnp.float32, jnp.bfloat16, jnp.int32
     dma = pltpu.SemaphoreType.DMA
-    small, ints = (4, 2, GROUPS, 128), (4, 3, GROUPS, 128)
+    small, ints = (4, 2, GROUPS, 128), (4, 2, GROUPS, 128)
     mat, square = ((TOK, DIM), bf16), ((ROWS, TOK), bf16)
     shapes = [((VOCAB, DIM), bf16), mat, ((TOK, VOCAB), f32), (small, f32), (ints, i32),
               mat, mat, mat, mat, square, square, square, ((DEFER - 1, ROWS, KT), bf16), ((ROWS, DIM), f32), ((4, 2, DIM), f32)]
@@ -744,19 +774,19 @@
         step_kernel,
         name="step",
         out_shape=[jax.ShapeDtypeStruct(s, d) for s, d in shapes],
-        in_specs=[any_spec, vmem_spec, vmem_spec, any_spec, any_spec],
+        in_specs=[any_spec, vmem_spec, vmem_spec, any_spec, vmem_spec, vmem_spec],
         out_specs=[any_spec] * len(shapes),
         scratch_shapes=[
-            pltpu.VMEM((3, GROUPS, 128), i32), pltpu.VMEM((2, GROUPS, 128), f32), pltpu.VMEM(small, f32), pltpu.VMEM(ints, i32),
+            pltpu.VMEM((GROUPS, 128), i32), pltpu.VMEM((2, GROUPS, 128), f32), pltpu.VMEM(small, f32), pltpu.VMEM(ints, i32),
             pltpu.VMEM((2, 8, DIM), f32), pltpu.VMEM((2, DIM), f32), pltpu.VMEM((8, DIM), f32),
             dma((2,)), dma, dma((2,)), dma((2,)), dma((2,)), dma((4,)), dma((2,)), dma((2,)), dma((2,)), dma, dma,
             dma, dma, dma, dma, dma, dma, dma, dma, dma, dma,
-            dma((CHUNKS,)), dma((CHUNKS,)), dma((TILES - NEAR,)), dma((ROWS // PE_ROWS,)), dma((4,)), dma((4,)),
+            dma((CHUNKS,)), dma((CHUNKS,)), dma((TILES - NEAR,)), dma((ROWS // PE_ROWS,)), dma((8,)), dma((4,)),
             dma((XCHS,)), dma((XCHS,)), dma, dma((4,)), dma((4,)),
         ],
         compiler_params=pltpu.CompilerParams(collective_id=0, has_side_effects=True, vmem_limit_bytes=67043328),
         cost_estimate=pl.CostEstimate(flops=12 * TOK * VOCAB * DIM, bytes_accessed=700 * 2 ** 20, transcendentals=3 * TOK * VOCAB),
-    )(hidden, gain, bias, embed, info)
+    )(hidden, gain, bias, embed, targets, mask)
 
 
 def finish_kernel(de_in, dzt_last, x_xp, x_xq, emb, dh_in, stat_all, info_all, gsum_all,
@@ -932,17 +962,7 @@
 
 def solution(mesh):
     def body(hidden, ln_gain, ln_bias, embed, targets, loss_mask):
-        dp, rank = lax.axis_index('dp'), lax.axis_index('tp')
-        shard = targets // ROWS
-        block = jnp.bitwise_xor(shard, rank)
-        row = targets % ROWS
-        half = row // (ROWS // 2)
-        sub = row % (ROWS // 2)
-        piece = (block - 2) * 2 + jnp.bitwise_xor(half, dp)
-        far = 2 * ROWS + (sub // PIECE_ROWS) * TILE + piece * PIECE_ROWS + sub % PIECE_ROWS
-        tcol = jnp.where(block < 2, block * ROWS + row, far)
-        info = jnp.stack([targets, loss_mask, tcol]).reshape(3, GROUPS, 128)
-        outs = run_step(hidden, ln_gain.reshape(1, DIM), ln_bias.reshape(1, DIM), embed, info)
+        outs = run_step(hidden, ln_gain.reshape(1, DIM), ln_bias.reshape(1, DIM), embed, targets.reshape(GROUPS, 128), loss_mask.reshape(GROUPS, 128))
         stat_all, info_all, dhid, x_xp, x_xq, dzt_last, de_part, gsum_all = (outs[i] for i in (3, 4, 5, 7, 8, 12, 13, 14))
         d_embed, d_hidden, loss, mean, d_gain, d_bias = finish(de_part, dzt_last, x_xp, x_xq, embed, dhid, stat_all, info_all, gsum_all)
         return loss.reshape(TOK), mean.reshape(1), d_hidden, d_embed, d_gain.reshape(DIM), d_bias.reshape(DIM)

time: 633 us -> 627 us (level)
  no operation moved by 1% of the time
where the time goes in v9:
time: 627 us
  Pallas kernels  626 us (100%)
    pallas_call x1, Pallas kernels, run_step(): pl.pallas_call(step_kernel, name='step', out_shape=[jax.ShapeDtypeStruct(...  569 us
    pallas_call x1, Pallas kernels, finish(): pl.pallas_call(finish_kernel, name='finish', out_shape=[jax.ShapeDtypeStr...  57.1 us

profile of v9, /device:TPU:0, one launch (start us, length us, event | category | flops | bytes accessed | tf_op | source)
XLA Modules:
  0.0 626.7 jit_solution(15349788834725897564)
XLA Ops:
  0.6 568.9 %step.1 = (bf16[8192,4096]{1,0:T(8,128)(2,1)}, bf16[2048,4096]{1,0:T(8,128)(2,1)}, f32[2048,8192]{1,0:T(8,128)}, f32[4,2,16,128]{3,2,1,0:T(8,128)}, s32[4,2,16,1...) custom-call(bf16[2048,4096]{1,0:T(8,128)(2,1)} %hid.1, ...), custom_call_target="tpu_custom_call" | custom-call | flops 824633720832 | bytes 734003200 | tf_op jit(solution)/shard_map/step/pallas_call | solution.py:773
  569.5 57.1 %finish.1 = (f32[2048,4096]{1,0:T(8,128)}, bf16[2048,4096]{1,0:T(8,128)(2,1)}, f32[16,128]{1,0:T(8,128)}, f32[1,1]{1,0:T(1,128)}, f32[1,4096]{1,0:T(1,128)}, /*index=5*/f32[1,4096]{1,0:T(1,128)}) custom-call(f32[2048,4096]{1,0:T(8,128)} %get-tuple-element.20.de_in, bf16[3,2048,512]{2,1,0:T(8,128)(2,1)} %get-tuple-element.21.dzt_last, ...), custom_call_target="tpu_custom_call" | custom-call | flops 42949672960 | bytes 136314880 | tf_op jit(solution)/shard_map/finish/pallas_call | solution.py:947

commit v10 on v9

--- a/solution.py
+++ b/solution.py
@@ -77,9 +77,9 @@
         pl.semaphore_signal(barrier, inc=1, device_id=dev, device_id_type=pl.DeviceIdType.MESH)
     pl.semaphore_wait(barrier, 4)
 
-    def info_copies():
-        return [remote(ref, info_all.at[tp, i], sm_send, info_recv.at[2 * p + i], dev)
-                for p, dev in group for i, ref in enumerate((targets, mask))]
+    def info_copies(i):
+        ref = (targets, mask)[i]
+        return [remote(ref, info_all.at[tp, i], sm_send, info_recv.at[2 * p + i], dev) for p, dev in group]
 
     def columns():
         for s in range(4):
@@ -137,13 +137,17 @@
             return pltpu.make_async_copy(hid.at[pl.ds(pl.multiple_of(i * LN_ROWS, LN_ROWS), LN_ROWS)], hbuf.at[lax.rem(i, 2)], h_sem.at[lax.rem(i, 2)])
         h_copy(0).start()
 
-        for cp in info_copies():
+        for j in range(2):
+            x_copy(j).start()
+        for cp in info_copies(1):
             cp.start()
 
         def start_x(j, c):
             x_copy(j).start()
             return c
-        lax.fori_loop(0, CHUNKS, start_x, 0)
+        lax.fori_loop(2, CHUNKS, start_x, 0)
+        for cp in info_copies(0):
+            cp.start()
 
         def start_pe(i, c):
             pe_copy(i).start()
@@ -188,9 +192,10 @@
                 h_copy(i + 1).start()
             h_copy(i).wait()
 
-            @pl.when(i == 6)
-            def _():
-                x_event(0)
+            for at, j in ((4, 0), (7, 1)):
+                @pl.when(i == at)
+                def _(j=j):
+                    x_event(j)
 
             def ln_rows(r, c2):
                 base = r * LN_UNROLL * 16
@@ -266,17 +271,20 @@
                 zs[h], z_out.at[pl.ds(h * HB, HB), pl.ds(pl.multiple_of(t * TILE, TILE), TILE)], z_sem.at[h])
 
         def start_events(t):
-            @pl.when(t < TILES - 1)
-            def _():
-                x_event(t + 1)
-
-            @pl.when(t == TILES - 2)
+            @pl.when(t < TILES - 2)
+            def _():
+                x_event(t + 2)
+
+            @pl.when(t == 0)
+            def _():
+                y_event(0)
+
+            @pl.when(t == TILES - 3)
             def _():
                 xt_copy(0).start()
 
             @pl.when(t == TILES - 1)
             def _():
-                y_event(TILES - 1)
                 p_event(TILES - 1 - NEAR)
             e_load(t).wait()
 
@@ -288,7 +296,7 @@
         def middle_events(t):
             @pl.when(t < TILES - 1)
             def _():
-                y_event(t)
+                y_event(t + 1)
 
             @pl.when((t >= 1) & (t < ROWS // TILE + 1))
             def _():
@@ -322,13 +330,15 @@
 
             @pl.when(t == NEAR + 1)
             def _():
-                for cp in info_copies():
+                for cp in info_copies(1):
                     cp.wait_recv()
                 for cp in own_info:
                     cp.wait()
-                load = pltpu.make_async_copy(info_all, infos, small_sem.at[0])
-                load.start()
-                load.wait()
+                loads = [pltpu.make_async_copy(info_all.at[q, 1], infos.at[q, 1], small_sem.at[0]) for q in range(4)]
+                for load in loads:
+                    load.start()
+                for load in loads:
+                    load.wait()
                 count = jnp.broadcast_to(token_count(), (1, 128))
                 for r in range(GROUPS):
                     spread(mask[r:r + 1, :].astype(f32) / count, slice(r * 128, (r + 1) * 128), scale_v)
@@ -648,9 +658,14 @@
             for p, dev in group:
                 remote(stat_v, stat_all.at[tp], sm_send, stat_recv.at[p], dev).wait_recv()
             pltpu.make_async_copy(stat_v, stat_all.at[tp], small_sem.at[1]).wait()
-            stat_load = pltpu.make_async_copy(stat_all, stats, small_sem.at[1])
-            stat_load.start()
-            stat_load.wait()
+            for cp in info_copies(0):
+                cp.wait_recv()
+            loads = [pltpu.make_async_copy(stat_all, stats, small_sem.at[1])]
+            loads += [pltpu.make_async_copy(info_all.at[q, 0], infos.at[q, 0], small_sem.at[0]) for q in range(4)]
+            for load in loads:
+                load.start()
+            for load in loads:
+                load.wait()
             count = jnp.broadcast_to(token_count(), (1, 128))
 
             def far(r, c):
@@ -754,7 +769,7 @@
     pltpu.make_async_copy(x_out, x_out, xd_send).wait()
     xp_copy.wait_send()
     pltpu.make_async_copy(dzt_out, dzt_out, dz_send).wait()
-    for cp in info_copies():
+    for cp in (*info_copies(0), *info_copies(1)):
         cp.wait_send()
     for p, dev in group:
         remote(stat_v, stat_all.at[tp], sm_send, stat_recv.at[p], dev).wait_send()

time: 627 us -> 626 us (level)
  no operation moved by 1% of the time
where the time goes in v10:
time: 626 us
  Pallas kernels  625 us (100%)
    pallas_call x1, Pallas kernels, run_step(): pl.pallas_call(step_kernel, name='step', out_shape=[jax.ShapeDtypeStruct(...  568 us
    pallas_call x1, Pallas kernels, finish(): pl.pallas_call(finish_kernel, name='finish', out_shape=[jax.ShapeDtypeStr...  57.1 us

profile of v10, /device:TPU:0, one launch (start us, length us, event | category | flops | bytes accessed | tf_op | source)
XLA Modules:
  0.0 625.9 jit_solution(15016485190687941376)
XLA Ops:
  0.6 568.0 %step.1 = (bf16[8192,4096]{1,0:T(8,128)(2,1)}, bf16[2048,4096]{1,0:T(8,128)(2,1)}, f32[2048,8192]{1,0:T(8,128)}, f32[4,2,16,128]{3,2,1,0:T(8,128)}, s32[4,2,16,1...) custom-call(bf16[2048,4096]{1,0:T(8,128)(2,1)} %hid.1, ...), custom_call_target="tpu_custom_call" | custom-call | flops 824633720832 | bytes 734003200 | tf_op jit(solution)/shard_map/step/pallas_call | solution.py:788
  568.6 57.1 %finish.1 = (f32[2048,4096]{1,0:T(8,128)}, bf16[2048,4096]{1,0:T(8,128)(2,1)}, f32[16,128]{1,0:T(8,128)}, f32[1,1]{1,0:T(1,128)}, f32[1,4096]{1,0:T(1,128)}, /*index=5*/f32[1,4096]{1,0:T(1,128)}) custom-call(f32[2048,4096]{1,0:T(8,128)} %get-tuple-element.20.de_in, bf16[3,2048,512]{2,1,0:T(8,128)(2,1)} %get-tuple-element.21.dzt_last, ...), custom_call_target="tpu_custom_call" | custom-call | flops 42949672960 | bytes 136314880 | tf_op jit(solution)/shard_map/finish/pallas_call | solution.py:962
